TPU v7x, 32 devices: a whole 2x2x4 slice. The times are simulated.
32 devices in a mesh: fsdp: 8 (over z, y), tp: 4 (over x, core).
Axes of the slice: x: 2, y: 2, z: 4, core: 2. Of those that a mesh axis runs over, the one named last changes fastest.
Arguments:
- hidden_in: bfloat16 [1024, 8192], P('fsdp'), may hold values from -6 to 6
- key_grad: bfloat16 [1024, 1024], P('fsdp', 'tp'), may hold values from -2.5 to 2.5
- positions: int32 [1024], P('fsdp'), may hold values from 0 to 1023, as said below
- key_quant: bfloat16 [8704, 1024], P('fsdp', 'tp'), may hold values from -4 to 4
- key_scales: float32 [8704, 8], P('fsdp', 'tp'), may hold values from 0.01 to 0.1
- block_counts: int32 [8], replicated, may hold values from 960 to 1088, as said below
Outputs:
- weight_grad: bfloat16 [8704, 1024], P('fsdp', 'tp')
- input_grad: bfloat16 [1024, 8192], P('fsdp', 'tp')
Inputs may be any that keep to these rules, and one draw needn't show every extreme that they name: Index f of fsdp owns the consecutive projection rows from block_counts[0] + ... + block_counts[f-1] on, in its first block_counts[f] slots; the counts sum to 8192, and some index owns exactly 1088 rows. positions count the tokens from the start of their packed document; the first token's document may have begun before the first token, and a document may go on into the next index's tokens.
All inputs are finite; a program needn't handle non-finite values.
Results may differ from a plain program's by a relative error of at most 0.013.
Values may be sent and summed in bfloat16 or wider, within the bound.
A program may use at most 64 MiB of HBM per device.

v0:
```python
import functools
import math

import jax
import jax.numpy as jnp
from jax import lax
from jax.experimental import pallas as pl
from jax.experimental.pallas import tpu as pltpu
from jax.sharding import PartitionSpec as P

HD = 128
LANES = 128
LINE = 2
MESH = pl.DeviceIdType.MESH

rope_base = 500000.0


def rotary_tables(positions):
    half_dim = HD // 2
    freq_idx = jnp.arange(half_dim, dtype=jnp.float32)
    inverse = jnp.exp(-(2.0 * freq_idx / HD) * math.log(rope_base))
    angles = positions.astype(jnp.float32)[:, None] * inverse[None, :]
    return jnp.cos(angles), jnp.sin(angles)


def offset_range(index, owners_n, row_total, slot_count):
    least_count = 2 * row_total // owners_n - slot_count
    later = owners_n - index
    least = max(index * least_count, row_total - later * slot_count)
    greatest = min(index * slot_count, row_total - later * least_count)
    return least, greatest


def exchange_fits(owners_n, group_total, slot_count, row_total, tokens_here, width):
    if group_total % 2 or owners_n % group_total or owners_n % LINE or slot_count % (16 * group_total):
        return False
    if tokens_here % LANES or width % LANES or row_total % group_total or (row_total // group_total) % LANES:
        return False
    quarter = slot_count // group_total
    chunk = row_total // group_total
    per_chunk = owners_n // group_total
    if 2 * row_total // owners_n - slot_count < quarter or row_total < 2 * quarter + 4 * LANES:
        return False
    for owner in range(owners_n):
        least, greatest = offset_range(owner, owners_n, row_total, slot_count)
        home = owner // per_chunk
        for part in range(group_total):
            reach = range(
                max(0, (least + part * quarter) // chunk),
                min(group_total - 1, (greatest + (part + 1) * quarter - 1) // chunk) + 1,
            )
            allowed = {home}
            if part == 0 and owner % per_chunk == 0:
                allowed.add(home - 1)
            if part == group_total - 1 and owner % per_chunk == per_chunk - 1:
                allowed.add(home + 1)
            if not set(reach) <= allowed:
                return False
    return True


def pick_kernel(owners_n, group_total, span, counts_ref, hidden_any, picked_ref, windows, shifted, load_sem):
    part = lax.axis_index("tp")
    row_total = hidden_any.shape[1]
    quarter = picked_ref.shape[1]
    offset = jnp.int32(0)
    plans = []
    for owner in range(owners_n):
        count = counts_ref[owner]
        start = jnp.minimum(offset + part * quarter, row_total)
        base = jnp.minimum((start // LANES) * LANES, row_total - span)
        load = pltpu.make_async_copy(
            hidden_any.at[:, pl.ds(pl.multiple_of(base, LANES), span)], windows.at[owner], load_sem.at[owner]
        )
        load.start()
        plans.append((count, start - base, load))
        offset = offset + count
    for owner, (count, shift, load) in enumerate(plans):
        load.wait()
        shifted[owner, pl.ds(0, span), :] = windows[owner].astype(jnp.float32).T
        moved = shifted[owner, pl.ds(shift, quarter), :]
        slot = lax.broadcasted_iota(jnp.int32, moved.shape, 0) + part * quarter
        picked_ref[owner] = jnp.where(slot < count, moved, 0.0).astype(jnp.bfloat16)


def assemble_kernel(owners_n, group_total, pad, counts_ref, pieces_ref, grad_ref, grad_out, out_ref, rows):
    chunk_at = lax.axis_index("tp")
    chunk = out_ref.shape[1]
    quarter = pieces_ref.shape[1]
    per_chunk = owners_n // group_total
    offsets = []
    offset = jnp.int32(0)
    for owner in range(owners_n):
        offsets.append(offset)
        offset = offset + counts_ref[owner]

    def first_row(owner):
        found = jnp.int32(0)
        for candidate in range(owners_n):
            found = jnp.where(owner == candidate, offsets[candidate], found)
        return found

    limit = rows.shape[0] - quarter

    def place(index, begin):
        rows[pl.ds(jnp.clip(begin, 0, limit), quarter), :] = pieces_ref[index].astype(jnp.float32)

    for part in range(group_total):
        grad_out[pl.ds(part * quarter, quarter), :] = grad_ref[part]
    origin = pad - chunk_at * chunk
    first = chunk_at * per_chunk
    below = first_row(first - 1) + (group_total - 1) * quarter + origin
    place(0, jnp.where(chunk_at > 0, below, 0))
    for near in range(per_chunk):
        start = first_row(first + near) + origin
        for part in range(group_total):
            place(1 + near * group_total + part, start + part * quarter)
    above = first_row(first + per_chunk) + origin
    last = 1 + per_chunk * group_total
    place(last, jnp.where(chunk_at < group_total - 1, above, limit))
    for at in range(0, chunk, LANES):
        out_ref[:, pl.ds(at, LANES)] = rows[pl.ds(pad + at, LANES), :].T.astype(jnp.bfloat16)


def exchange_kernel(
    owners_n, group_total, picked_ref, grad_ref, cos_ref, sin_ref, quant_ref, scales_ref,
    grad_out, pieces_out,
    rot_ref, weights_ref,
    rotated, weights, hidden, outgoing, grad_send,
    own_sem, tp_send, tp_recv, w_send, w_recv, h_send, h_recv,
    up_send, down_send, side_send, pair_send, net_recv, pair_recv,
    o_send, e_send, o_recv, g_send, g_recv, local_sem,
):
    here = lax.axis_index("fsdp")
    part = lax.axis_index("tp")
    core = lax.rem(part, 2)
    partner = part + 1 - 2 * core
    tokens, width = rot_ref.shape
    quarter = picked_ref.shape[1]
    half = width * group_total // 2
    pieces = group_total // 2
    depth = owners_n // LINE
    z = here // LINE
    y = lax.rem(here, LINE)
    beside = z * LINE + (1 - y)
    per_chunk = owners_n // group_total
    home = here // per_chunk
    last_piece = 1 + per_chunk * group_total

    def remote(src, dst, send, recv, where):
        return pltpu.make_async_remote_copy(
            src_ref=src, dst_ref=dst, send_sem=send, recv_sem=recv, device_id=where, device_id_type=MESH
        )

    def rows_of(owner):
        return pl.ds(pl.multiple_of(owner * tokens, tokens), tokens)

    def cols_of(group):
        return pl.ds(pl.multiple_of(group * width, width), width)

    def slots_of(group):
        return pl.ds(pl.multiple_of(group * quarter, 16), quarter)

    def spread(step):
        target = lax.rem(part + step, group_total)
        block = rotated.at[rows_of(here), cols_of(part)]
        return remote(rot_ref, block, tp_send.at[step - 1], tp_recv.at[step - 1], (here, target))

    def weigh(step):
        target = lax.rem(part + step, group_total)
        return remote(
            weights_ref.at[slots_of(target), :], weights.at[:, cols_of(part)],
            w_send.at[step - 1], w_recv.at[step - 1], (here, target),
        )

    def hide(target):
        return remote(
            picked_ref.at[target], hidden.at[:, rows_of(here)],
            h_send.at[target], h_recv.at[here], (target, part),
        )

    def hidden_from(owner):
        return remote(
            picked_ref.at[owner], hidden.at[:, rows_of(owner)],
            h_send.at[owner], h_recv.at[owner], (owner, part),
        )

    def block_of(owner, piece):
        first = core * half + piece * width
        return rotated.at[rows_of(owner), pl.ds(pl.multiple_of(first, LANES), width)]

    def relay(owner, send, where, piece):
        view, at = block_of(owner, piece), owner * pieces + piece
        return remote(view, view, send.at[at], net_recv.at[at], (where, part))

    def share(owner, piece):
        view, at = block_of(owner, piece), owner * pieces + piece
        return remote(view, view, pair_send.at[at], pair_recv.at[at], (here, partner))

    own_rot = pltpu.make_async_copy(rot_ref, rotated.at[rows_of(here), cols_of(part)], own_sem.at[0])
    own_weights = pltpu.make_async_copy(
        weights_ref.at[slots_of(part), :], weights.at[:, cols_of(part)], own_sem.at[1]
    )
    own_hidden = pltpu.make_async_copy(picked_ref.at[here], hidden.at[:, rows_of(here)], own_sem.at[2])
    own_hidden.start()
    heads = scales_ref.shape[0]
    cosine = jnp.concatenate([cos_ref[...], cos_ref[...]], axis=1)
    sine = jnp.concatenate([sin_ref[...], -sin_ref[...]], axis=1)
    for head in range(heads):
        cols = pl.ds(head * HD, HD)
        values = grad_ref[:, cols].astype(jnp.float32)
        swapped = jnp.concatenate([values[:, HD // 2 :], values[:, : HD // 2]], axis=1)
        rot_ref[:, cols] = (values * cosine + swapped * sine).astype(jnp.bfloat16)
    for head in range(heads):
        cols = pl.ds(head * HD, HD)
        scale = jnp.broadcast_to(scales_ref[head : head + 1, :], (HD, scales_ref.shape[1])).T
        weights_ref[:, cols] = (quant_ref[:, cols].astype(jnp.float32) * scale).astype(jnp.bfloat16)
        if head == 0:
            hide(beside).start()
            own_rot.start()
            for step in range(1, group_total):
                spread(step).start()
    own_weights.start()
    for step in range(1, group_total):
        weigh(step).start()

    def hide_at(rise, across):
        level = z + rise

        @pl.when((level >= 0) & (level < depth))
        def _():
            hide(level * LINE + (1 - y if across else y)).start()

    own_rot.wait()
    for step in range(1, group_total):
        spread(step).wait_recv()

    below, above = here - LINE, here + LINE

    def travel(owner, go_up, go_down, act, piece):
        @pl.when(go_up)
        def _():
            act(relay(owner, up_send, above, piece))

        @pl.when(go_down)
        def _():
            act(relay(owner, down_send, below, piece))

    def begin(copy):
        copy.start()

    def finish(copy):
        copy.wait_send()

    def send_piece(owner, act_remote, act_local):
        source = outgoing.at[owner]

        def give(to_chunk, index, send, slot):
            mine = (owner == here) & (to_chunk == part)

            @pl.when(jnp.logical_not(mine))
            def _():
                act_remote(remote(source, pieces_out.at[index], send, o_recv.at[index], (owner, to_chunk)))

            @pl.when(mine)
            def _():
                act_local(pltpu.make_async_copy(source, pieces_out.at[index], local_sem.at[slot]))

        near = lax.rem(here, per_chunk)
        give(home, 1 + near * group_total + part, o_send.at[owner], 0)

        @pl.when((near == per_chunk - 1) & (part == group_total - 1) & (home < group_total - 1))
        def _():
            give(home + 1, 0, e_send.at[owner], 1)

        @pl.when((near == 0) & (part == 0) & (home > 0))
        def _():
            give(home - 1, last_piece, e_send.at[owner], 1)

    for piece in range(pieces):
        travel(here, z < depth - 1, z > 0, begin, piece)
        relay(here, side_send, beside, piece).start()
    hide_at(1, False)
    hide_at(-1, False)

    def produce(owner):
        outgoing[owner] = lax.dot_general(
            weights[...], rotated[rows_of(owner), :], (((1,), (1,)), ((), ())),
            preferred_element_type=jnp.float32,
        ).astype(jnp.bfloat16)

    def stage_items(away):
        items = []
        for sign in (-1, 1):
            if 0 < away < depth:
                items.append((z + sign * away, y))
            if away > 1 or (away == 1 and sign < 0):
                items.append((z + sign * (away - 1), 1 - y))
        return items

    for away in range(1, depth + 2):
        for sign in (-1, 1):
            if away < depth:
                level = z + sign * away
                owner = level * LINE + y

                @pl.when((level >= 0) & (level < depth))
                def _():
                    for piece in range(pieces):
                        relay(owner, up_send, here, piece).wait_recv()
                        if sign < 0:
                            travel(owner, z < depth - 1, z < 0, begin, piece)
                        else:
                            travel(owner, z < 0, z > 0, begin, piece)
                        relay(owner, side_send, beside, piece).start()
                        share(owner, piece).start()

            if away <= depth and (away > 1 or sign < 0):
                level_near = z + sign * (away - 1)
                other = level_near * LINE + (1 - y)

                @pl.when((level_near >= 0) & (level_near < depth))
                def _():
                    for piece in range(pieces):
                        relay(other, up_send, here, piece).wait_recv()
                        share(other, piece).start()

        if away < depth:
            hide_at(away, True)
            hide_at(-away, True)
        if away + 1 < depth:
            hide_at(away + 1, False)
            hide_at(-away - 1, False)
        if away == 2:
            own_weights.wait()
            for step in range(1, group_total):
                weigh(step).wait_recv()
            produce(here)
            send_piece(here, begin, begin)
        ready = stage_items(away - 1)
        for level, row in ready:

            @pl.when((level >= 0) & (level < depth))
            def _():
                for piece in range(pieces):
                    share(level * LINE + row, piece).wait_recv()
                produce(level * LINE + row)

        for level, row in ready:

            @pl.when((level >= 0) & (level < depth))
            def _():
                send_piece(level * LINE + row, begin, begin)

    own_hidden.wait()
    for step in range(1, owners_n):
        hidden_from(lax.rem(here + step, owners_n)).wait_recv()

    def send_grad(step):
        target = lax.rem(part + step, group_total)
        return remote(
            grad_send.at[target], grad_out.at[part], g_send.at[step - 1], g_recv.at[step - 1], (here, target)
        )

    def reduce(step, carry):
        target = lax.rem(part + step, group_total)
        grad_send[target] = jnp.dot(
            hidden[...], rotated[:, cols_of(target)], preferred_element_type=jnp.float32
        ).astype(jnp.bfloat16)

        @pl.when(step > 1)
        def _():
            send_grad(step - 1).start()

        return carry

    lax.fori_loop(1, group_total + 1, reduce, 0)
    own_grad = pltpu.make_async_copy(grad_send.at[part], grad_out.at[part], own_sem.at[3])
    own_grad.start()

    for owner in range(owners_n):
        send_piece(jnp.int32(owner), finish, lambda copy: copy.wait())
    for near in range(per_chunk):
        for source in range(group_total):
            index = 1 + near * group_total + source

            @pl.when(jnp.logical_not((home == part) & (here == part * per_chunk + near) & (part == source)))
            def _():
                remote(outgoing.at[0], pieces_out.at[index], o_send.at[0], o_recv.at[index], (here, partner)).wait_recv()

    for index, exists, mine in (
        (0, part > 0, (here == part * per_chunk - 1) & (part == group_total - 1)),
        (last_piece, part < group_total - 1, (here == (part + 1) * per_chunk) & (part == 0)),
    ):

        @pl.when(exists & jnp.logical_not(mine))
        def _():
            remote(outgoing.at[0], pieces_out.at[index], o_send.at[0], o_recv.at[index], (here, partner)).wait_recv()

    own_grad.wait()
    for step in range(1, group_total):
        send_grad(step).wait_send()
        remote(grad_send.at[0], grad_out.at[0], g_send.at[step - 1], g_recv.at[step - 1], (here, partner)).wait_recv()
    for step in range(1, group_total):
        spread(step).wait_send()
        weigh(step).wait_send()
    for step in range(1, owners_n):
        hide(lax.rem(here + step, owners_n)).wait_send()
    for piece in range(pieces):
        travel(here, z < depth - 1, z > 0, finish, piece)
        relay(here, side_send, beside, piece).wait_send()
    for away in range(1, depth):
        for sign in (-1, 1):
            level = z + sign * away
            owner = level * LINE + y

            @pl.when((level >= 0) & (level < depth))
            def _():
                for piece in range(pieces):
                    if sign < 0:
                        travel(owner, z < depth - 1, z < 0, finish, piece)
                    else:
                        travel(owner, z < 0, z > 0, finish, piece)
                    relay(owner, side_send, beside, piece).wait_send()

    def drain(step, carry):
        for piece in range(pieces):
            share(lax.rem(here + step, owners_n), piece).wait_send()
        return carry

    lax.fori_loop(1, owners_n, drain, 0)


def exchange_plan(hidden_in, key_grad, positions, key_quant, key_scales, block_counts):
    owners_n = lax.axis_size("fsdp")
    group_total = lax.axis_size("tp")
    slot_count, width = key_quant.shape
    tokens_here, row_total = hidden_in.shape
    quarter = slot_count // group_total
    chunk = row_total // group_total
    per_chunk = owners_n // group_total
    columns = width * group_total
    vmem = pl.BlockSpec(memory_space=pltpu.VMEM)
    anywhere = pl.BlockSpec(memory_space=pl.ANY)
    smem = pl.BlockSpec(memory_space=pltpu.SMEM)
    span = -(-(quarter + LANES) // LANES) * LANES
    cosine, sine = rotary_tables(positions)
    picked = pl.pallas_call(
        functools.partial(pick_kernel, owners_n, group_total, span),
        out_shape=jax.ShapeDtypeStruct((owners_n, quarter, tokens_here), jnp.bfloat16),
        in_specs=[smem, anywhere],
        out_specs=vmem,
        scratch_shapes=[
            pltpu.VMEM((owners_n, tokens_here, span), jnp.bfloat16),
            pltpu.VMEM((owners_n, 2 * span + quarter, tokens_here), jnp.float32),
            pltpu.SemaphoreType.DMA((owners_n,)),
        ],
        name="pick",
    )(block_counts, hidden_in)

    relays_n = owners_n * group_total // 2
    pieces_n = 2 + per_chunk * group_total
    dma = pltpu.SemaphoreType.DMA
    weight_grad, pieces = pl.pallas_call(
        functools.partial(exchange_kernel, owners_n, group_total),
        out_shape=(
            jax.ShapeDtypeStruct((group_total, quarter, width), jnp.bfloat16),
            jax.ShapeDtypeStruct((pieces_n, quarter, tokens_here), jnp.bfloat16),
        ),
        in_specs=[vmem] * 6,
        out_specs=(vmem,) * 2,
        scratch_shapes=[
            pltpu.VMEM((tokens_here, width), jnp.bfloat16),
            pltpu.VMEM((slot_count, width), jnp.bfloat16),
            pltpu.VMEM((owners_n * tokens_here, columns), jnp.bfloat16),
            pltpu.VMEM((quarter, columns), jnp.bfloat16),
            pltpu.VMEM((quarter, owners_n * tokens_here), jnp.bfloat16),
            pltpu.VMEM((owners_n, quarter, tokens_here), jnp.bfloat16),
            pltpu.VMEM((group_total, quarter, width), jnp.bfloat16),
            dma((4,)),
            dma((group_total - 1,)), dma((group_total - 1,)),
            dma((group_total - 1,)), dma((group_total - 1,)),
            dma((owners_n,)), dma((owners_n,)),
            dma((relays_n,)), dma((relays_n,)), dma((relays_n,)), dma((relays_n,)),
            dma((relays_n,)), dma((relays_n,)),
            dma((owners_n,)), dma((owners_n,)), dma((pieces_n,)),
            dma((group_total - 1,)), dma((group_total - 1,)),
            dma((2,)),
        ],
        compiler_params=pltpu.CompilerParams(has_side_effects=True),
        name="exchange",
    )(picked, key_grad, cosine, sine, key_quant, key_scales.T)

    margin = max(
        max(
            chunk * (owner // per_chunk) - offset_range(owner - 1, owners_n, row_total, slot_count)[0]
            for owner in range(per_chunk, owners_n, per_chunk)
        ),
        2 * quarter,
    ) if group_total > 1 else 2 * quarter
    pad = -(-(margin + slot_count) // 8) * 8
    return pl.pallas_call(
        functools.partial(assemble_kernel, owners_n, group_total, pad),
        out_shape=(
            jax.ShapeDtypeStruct((slot_count, width), jnp.bfloat16),
            jax.ShapeDtypeStruct((tokens_here, chunk), jnp.bfloat16),
        ),
        in_specs=[smem, vmem, vmem],
        out_specs=(vmem,) * 2,
        scratch_shapes=[pltpu.VMEM((chunk + 2 * pad, tokens_here), jnp.float32)],
        name="assemble",
    )(block_counts, pieces, weight_grad)


def rotary_backward(key_grad, positions):
    tokens_here = key_grad.shape[0]
    half_dim = HD // 2
    cotangent = key_grad.astype(jnp.float32).reshape(tokens_here, -1, HD)
    freq_idx = jnp.arange(half_dim, dtype=jnp.float32)
    inverse = jnp.exp(-(2.0 * freq_idx / HD) * math.log(rope_base))
    angles = positions.astype(jnp.float32)[:, None] * inverse[None, :]
    cosine = jnp.cos(angles)[:, None, :]
    sine_part = jnp.sin(angles)[:, None, :]
    lower_half = cotangent[..., :half_dim]
    upper_half = cotangent[..., half_dim:]
    back_lower = lower_half * cosine + upper_half * sine_part
    back_upper = upper_half * cosine - lower_half * sine_part
    joined = jnp.concatenate([back_lower, back_upper], axis=-1)
    return joined.reshape(tokens_here, -1).astype(jnp.bfloat16)


def slot_tables(block_counts, slot_count, row_total):
    offsets = jnp.cumsum(block_counts) - block_counts
    owners_n = block_counts.shape[0]
    slot_ids = jnp.arange(owners_n * slot_count, dtype=jnp.int32)
    within = slot_ids % slot_count
    live_counts = jnp.broadcast_to(block_counts[:, None], (owners_n, slot_count)).reshape(-1)
    base_rows = jnp.broadcast_to(offsets[:, None], (owners_n, slot_count)).reshape(-1)
    is_live = within < live_counts
    row_of_slot = jnp.where(is_live, base_rows + within, 0)
    row_ids = jnp.arange(row_total, dtype=jnp.int32)
    at_or_after = row_ids[:, None] >= offsets[None, :]
    owner_of_row = jnp.sum(at_or_after.astype(jnp.int32), axis=1) - 1
    row_begin = jnp.max(jnp.where(at_or_after, offsets[None, :], 0), axis=1)
    slot_of_row = owner_of_row * slot_count + row_ids - row_begin
    return (row_of_slot, is_live, slot_of_row)


def gather_plan(hidden_in, key_grad, positions, key_quant, key_scales, block_counts):
    slot_count = key_quant.shape[0]
    local_heads = key_scales.shape[1]
    row_total = hidden_in.shape[1]
    row_of_slot, is_live, slot_of_row = slot_tables(block_counts, slot_count, row_total)
    scaled = (
        key_quant.astype(jnp.float32).reshape(slot_count, local_heads, HD) * key_scales[:, :, None]
    )
    local_weights = scaled.astype(jnp.bfloat16).reshape(slot_count, local_heads * HD)
    rotated = rotary_backward(key_grad, positions)
    picked = jnp.where(
        is_live[None, :], jnp.take(hidden_in, row_of_slot, axis=1), jnp.zeros((), jnp.bfloat16)
    )
    weight_grad = lax.psum_scatter(
        lax.dot_general(
            picked, rotated, (((0,), (0,)), ((), ())), preferred_element_type=jnp.float32
        ),
        "fsdp",
        scatter_dimension=0,
        tiled=True,
    ).astype(jnp.bfloat16)
    group_total = lax.axis_size("tp")
    whole_slots = lax.all_gather(local_weights, "fsdp", axis=0, tiled=True)
    ordered = jnp.take(whole_slots, slot_of_row, axis=0)
    own_rows = lax.all_to_all(ordered, "tp", split_axis=0, concat_axis=1, tiled=True)
    all_heads = lax.all_gather(rotated, "tp", axis=1, tiled=True)
    tokens_here = all_heads.shape[0]
    feature_here = own_rows.shape[0]
    heads_grouped = all_heads.reshape(tokens_here, group_total, -1)
    rows_grouped = own_rows.reshape(feature_here, group_total, -1)
    group_part = jnp.einsum(
        "tgk,dgk->gtd", heads_grouped, rows_grouped, preferred_element_type=jnp.float32
    ).astype(jnp.bfloat16)
    input_grad = jnp.sum(group_part.astype(jnp.float32), axis=0).astype(jnp.bfloat16)
    return (weight_grad, input_grad)


def per_device(hidden_in, key_grad, positions, key_quant, key_scales, block_counts):
    tokens_here, row_total = hidden_in.shape
    slot_count, width = key_quant.shape
    fits = exchange_fits(
        lax.axis_size("fsdp"), lax.axis_size("tp"), slot_count, row_total, tokens_here, width
    )
    plan = exchange_plan if fits else gather_plan
    return plan(hidden_in, key_grad, positions, key_quant, key_scales, block_counts)


def solution(mesh):
    in_specs = (P("fsdp", None), P("fsdp", "tp"), P("fsdp"), P("fsdp", "tp"), P("fsdp", "tp"), P())
    out_specs = (P("fsdp", "tp"), P("fsdp", "tp"))
    return jax.shard_map(
        per_device, mesh=mesh, in_specs=in_specs, out_specs=out_specs, check_vma=False
    )
```

profile of v0, /device:TPU:1, one launch (start us, length us, event | category | flops | bytes accessed | tf_op | source)
XLA Modules:
  0.0 63.0 jit_solution(11418824652046268486)
XLA Ops:
  0.6 0.7 %convert_element_type.3 = f32[128]{0:T(128)S(1)} convert(s32[128]{0:T(128)} %param.8) | non-fusion elementwise | flops 128 | bytes 1024 | tf_op jit(solution)/shard_map/convert_element_type | solution.py:23
  1.3 1.0 %multiply_sine_fusion = (f32[128,64]{1,0:T(8,128)}, f32[128,64]{1,0:T(8,128)}) fusion(f32[64]{0:T(128)S(1)} %multiply_exponential_fusion, f32[128]{0:T(128)S(1)} %convert_element_type.3), kind=kLoop, calls=%fused_computation | loop fusion | flops 8192 | bytes 66304 | tf_op jit(solution)/shard_map/sin | solution.py:24
  2.3 3.4 %pick.1.picked_ref = bf16[8,272,128]{2,1,0:T(8,128)(2,1)} custom-call(s32[8]{0:T(128)} %counts_ref.3, bf16[128,8192]{1,0:T(8,128)(2,1)} %hidden_any.1), custom_call_target="tpu_custom_call" | custom-call | tf_op jit(solution)/shard_map/pick/pallas_call | solution.py:449
  5.7 54.7 %exchange.1 = (bf16[4,272,256]{2,1,0:T(8,128)(2,1)}, bf16[10,272,128]{2,1,0:T(8,128)(2,1)}) custom-call(bf16[8,272,128]{2,1,0:T(8,128)(2,1)} %pick.1.picked_ref, bf16[128,256]{1,0:T(8,128)(2,1)} %grad_ref.1, f32[128,64]{1,0:T(8,128)} %get-tuple-element.7.cos_ref, f32[128,64]{1,0:T(8,128)} %get-tuple-element.6.sin_ref, bf16[1088,256]{1,0:T(8,128)(2,1)} %quant_ref.1, ...), custom_call_target="tpu_custom_call" | custom-call | tf_op jit(solution)/shard_map/exchange/pallas_call | solution.py:465
  60.4 2.5 %assemble.1 = (bf16[1088,256]{1,0:T(8,128)(2,1)}, bf16[128,2048]{1,0:T(8,128)(2,1)}) custom-call(s32[8]{0:T(128)} %counts_ref.3, bf16[10,272,128]{2,1,0:T(8,128)(2,1)} %get-tuple-element.4.pieces_ref, bf16[4,272,256]{2,1,0:T(8,128)(2,1)} %get-tuple-element.5.grad_ref), custom_call_target="tpu_custom_call" | custom-call | tf_op jit(solution)/shard_map/assemble/pallas_call | solution.py:503
  (1 shorter events, 0.0 us)
where the time goes:
time: 63.4 us; the launch traced here: 63 us
  Pallas kernels  60.7 us (96%)
  other arithmetic  1.62 us (3%)
  between operations  0.65 us (1%)
    pallas_call x1, Pallas kernels, exchange_plan(): pl.pallas_call(functools.partial(exchange_kernel, owners_n, group_total),...  54.7 us
    pallas_call x1, Pallas kernels, exchange_plan(): pl.pallas_call(functools.partial(pick_kernel, owners_n, group_total, span...  3.43 us
    pallas_call x1, Pallas kernels, exchange_plan(): pl.pallas_call(functools.partial(assemble_kernel, owners_n, group_total,...  2.54 us

commit v1 on v0

v1 whole, which is shorter than its diff:
```python
import functools
import math

import jax
import jax.numpy as jnp
from jax import lax
from jax.experimental import pallas as pl
from jax.experimental.pallas import tpu as pltpu
from jax.sharding import PartitionSpec as P

HD = 128
LANES = 128
LINE = 2
LOADS = 4
HIDE_EACH = 2
MESH = pl.DeviceIdType.MESH

rope_base = 500000.0


def offset_range(index, owners_n, row_total, slot_count):
    least_count = 2 * row_total // owners_n - slot_count
    later = owners_n - index
    least = max(index * least_count, row_total - later * slot_count)
    greatest = min(index * slot_count, row_total - later * least_count)
    return least, greatest


def exchange_fits(owners_n, group_total, slot_count, row_total, tokens_here, width):
    if group_total != 2 * LINE or owners_n % group_total or owners_n % LINE or slot_count % (16 * group_total):
        return False
    if tokens_here % LANES or width % LANES or row_total % group_total or (row_total // group_total) % LANES:
        return False
    quarter = slot_count // group_total
    chunk = row_total // group_total
    per_chunk = owners_n // group_total
    if 2 * row_total // owners_n - slot_count < quarter or row_total < 2 * quarter + 4 * LANES:
        return False
    for owner in range(owners_n):
        least, greatest = offset_range(owner, owners_n, row_total, slot_count)
        home = owner // per_chunk
        if greatest - least + quarter + 2 * LANES > row_total:
            return False
        for part in range(group_total):
            reach = range(
                max(0, (least + part * quarter) // chunk),
                min(group_total - 1, (greatest + (part + 1) * quarter - 1) // chunk) + 1,
            )
            allowed = {home}
            if part == 0 and owner % per_chunk == 0:
                allowed.add(home - 1)
            if part == group_total - 1 and owner % per_chunk == per_chunk - 1:
                allowed.add(home + 1)
            if not set(reach) <= allowed:
                return False
    return True


def assemble_kernel(owners_n, group_total, pad, counts_ref, pieces_ref, grad_ref, grad_out, out_ref, rows):
    chunk_at = lax.axis_index("tp")
    chunk = out_ref.shape[1]
    quarter = pieces_ref.shape[1]
    per_chunk = owners_n // group_total
    offsets = []
    offset = jnp.int32(0)
    for owner in range(owners_n):
        offsets.append(offset)
        offset = offset + counts_ref[owner]

    def first_row(owner):
        found = jnp.int32(0)
        for candidate in range(owners_n):
            found = jnp.where(owner == candidate, offsets[candidate], found)
        return found

    limit = rows.shape[0] - quarter

    def place(index, begin):
        rows[pl.ds(jnp.clip(begin, 0, limit), quarter), :] = pieces_ref[index].astype(jnp.float32)

    for part in range(group_total):
        grad_out[pl.ds(part * quarter, quarter), :] = grad_ref[part]
    origin = pad - chunk_at * chunk
    first = chunk_at * per_chunk
    below = first_row(first - 1) + (group_total - 1) * quarter + origin
    place(0, jnp.where(chunk_at > 0, below, 0))
    for near in range(per_chunk):
        start = first_row(first + near) + origin
        for part in range(group_total):
            place(1 + near * group_total + part, start + part * quarter)
    above = first_row(first + per_chunk) + origin
    last = 1 + per_chunk * group_total
    place(last, jnp.where(chunk_at < group_total - 1, above, limit))
    for at in range(0, chunk, LANES):
        out_ref[:, pl.ds(at, LANES)] = rows[pl.ds(pad + at, LANES), :].T.astype(jnp.bfloat16)


def exchange_kernel(
    owners_n, group_total, counts_ref, hidden_any, grad_any, positions_any, quant_any, scales_any,
    grad_out, pieces_out,
    hidden_in, grad_ref, positions_ref, quant_ref, scales_ref,
    weights_ref, rotated, weights, picked, hidden, outgoing, grad_send,
    load_sem, w_send, w_recv, h_send, h_recv,
    up_send, down_send, x_send, y_send, net_recv, pair_send, pair_recv,
    o_send, e_send, o_recv, g_send, g_recv,
):
    here = lax.axis_index("fsdp")
    part = lax.axis_index("tp")
    core = lax.rem(part, 2)
    side = part // 2
    partner = part + 1 - 2 * core
    across = lax.rem(part + 2, group_total)
    tokens, width = grad_ref.shape
    row_total = hidden_in.shape[1]
    quarter = picked.shape[1]
    depth = owners_n // LINE
    z = here // LINE
    y = lax.rem(here, LINE)
    beside = z * LINE + (1 - y)
    per_chunk = owners_n // group_total
    home = here // per_chunk
    last_piece = 1 + per_chunk * group_total

    loads = [pltpu.make_async_copy(grad_any, grad_ref, load_sem.at[0])]
    loads.append(pltpu.make_async_copy(positions_any, positions_ref, load_sem.at[1]))
    columns_each = row_total // LOADS
    for at in range(LOADS):
        columns = pl.ds(at * columns_each, columns_each)
        loads.append(
            pltpu.make_async_copy(hidden_any.at[:, columns], hidden_in.at[:, columns], load_sem.at[4 + at])
        )
    loads.append(pltpu.make_async_copy(quant_any, quant_ref, load_sem.at[2]))
    loads.append(pltpu.make_async_copy(scales_any, scales_ref, load_sem.at[3]))
    for load in loads:
        load.start()
    barrier = pltpu.get_barrier_semaphore()
    for step in range(owners_n):
        for turn in range(group_total):
            if step or turn:
                where = (lax.rem(here + step, owners_n), lax.rem(part + turn, group_total))
                pl.semaphore_signal(barrier, inc=1, device_id=where, device_id_type=MESH)

    def remote(src, dst, send, recv, where):
        return pltpu.make_async_remote_copy(
            src_ref=src, dst_ref=dst, send_sem=send, recv_sem=recv, device_id=where, device_id_type=MESH
        )

    def rows_of(owner):
        return pl.ds(pl.multiple_of(owner * tokens, tokens), tokens)

    def cols_of(group):
        return pl.ds(pl.multiple_of(group * width, width), width)

    def slots_of(group):
        return pl.ds(pl.multiple_of(group * quarter, 16), quarter)

    def weigh(step):
        target = lax.rem(part + step, group_total)
        return remote(
            weights_ref.at[slots_of(target), :], weights.at[:, cols_of(part)],
            w_send.at[step - 1], w_recv.at[step - 1], (here, target),
        )

    def hide(target):
        return remote(
            picked.at[target], hidden.at[:, rows_of(here)],
            h_send.at[target], h_recv.at[here], (target, part),
        )

    def hidden_from(owner):
        return remote(
            picked.at[owner], hidden.at[:, rows_of(owner)],
            h_send.at[owner], h_recv.at[owner], (owner, part),
        )

    def block(owner, row, lane):
        return rotated.at[rows_of(owner), cols_of(2 * row + lane)]

    def relay(owner, row, send, where):
        view = block(owner, row, core)
        return remote(view, view, send, net_recv.at[owner * 2 + row], where)

    def share(owner, row, lane):
        view, at = block(owner, row, lane), owner * 2 + row
        return remote(view, view, pair_send.at[at], pair_recv.at[at], (here, partner))

    offsets = []
    offset = jnp.int32(0)
    for owner in range(owners_n):
        offsets.append(offset)
        offset = offset + counts_ref[owner]

    def pick(owner):
        least, greatest = offset_range(owner, owners_n, row_total, quarter * group_total)
        span = -(-(greatest - least + quarter + LANES) // LANES) * LANES
        base = jnp.minimum((least + part * quarter) // LANES * LANES, row_total - span)
        window = hidden_in[:, pl.ds(pl.multiple_of(base, LANES), span)]
        slot = lax.broadcasted_iota(jnp.int32, (quarter, span), 0)
        column = lax.broadcasted_iota(jnp.int32, (quarter, span), 1)
        first = offsets[owner] + part * quarter - base
        live = jnp.minimum(first + counts_ref[owner] - part * quarter, span)
        chosen = (column == slot + first) & (column < live)
        moved = lax.dot_general(
            chosen.astype(jnp.float32).astype(jnp.bfloat16), window, (((1,), (1,)), ((), ())),
            preferred_element_type=jnp.float32,
        )
        picked[owner] = moved.astype(jnp.bfloat16)

    loads[0].wait()
    loads[1].wait()
    heads = scales_ref.shape[0]
    lane = lax.broadcasted_iota(jnp.int32, (tokens, HD), 1)
    pair_at = jnp.where(lane < HD // 2, lane, lane - HD // 2).astype(jnp.float32)
    inverse = jnp.exp(-(2.0 * pair_at / HD) * math.log(rope_base))
    place = jnp.broadcast_to(positions_ref[...].astype(jnp.float32), (HD, tokens)).T
    angles = place * inverse
    cosine = jnp.cos(angles)
    sine = jnp.sin(angles)
    sine = jnp.where(lane < HD // 2, sine, -sine)
    for head in range(heads):
        values = grad_ref[:, pl.ds(head * HD, HD)].astype(jnp.float32)
        swapped = jnp.concatenate([values[:, HD // 2 :], values[:, : HD // 2]], axis=1)
        cols = pl.ds(pl.multiple_of(part * width + head * HD, HD), HD)
        rotated[rows_of(here), cols] = (values * cosine + swapped * sine).astype(jnp.bfloat16)
    for load in loads[2 : 2 + LOADS]:
        load.wait()
    order = []
    for low in range((depth + 1) // 2):
        for level in dict.fromkeys((depth - 1 - low, low)):
            order += [level * LINE + row for row in range(LINE)]
    for owner in order[: 2 * LINE]:
        pick(owner)
    with jax.named_scope("barrier"):
        pl.semaphore_wait(barrier, owners_n * group_total - 1)

    def begin(copy):
        copy.start()

    def finish(copy):
        copy.wait_send()

    def from_z(level, up, down, act):
        owner = level * LINE + y

        @pl.when(up)
        def _():
            act(relay(owner, side, up_send.at[owner], (here + LINE, part)))

        @pl.when(down)
        def _():
            act(relay(owner, side, down_send.at[owner], (here - LINE, part)))

        act(relay(owner, side, x_send.at[owner], (here, across)))
        act(relay(owner, side, y_send.at[owner * 2 + side], (beside, part)))
        act(share(owner, side, core))

    def from_x(level, act):
        owner = level * LINE + y
        act(relay(owner, 1 - side, y_send.at[owner * 2 + 1 - side], (beside, part)))
        act(share(owner, 1 - side, core))

    def from_y(level, row, act):
        act(share(level * LINE + 1 - y, row, core))

    def arrived(owner, row):
        relay(owner, row, x_send.at[0], (here, across)).wait_recv()

    def levels(away):
        for sign in (-1, 1) if away else (1,):
            yield sign, z + sign * away

    def at_levels(away, act):
        if 0 <= away < depth:
            for sign, level in levels(away):

                @pl.when((level >= 0) & (level < depth))
                def _():
                    act(sign, level)

    def hide_item(item):
        level, row = item // LINE, (1 - y if item % LINE == 0 else y)
        above = depth - 1 - level

        @pl.when(above > z)
        def _():
            hide(above * LINE + row).start()

        @pl.when(level < z)
        def _():
            hide(level * LINE + row).start()

    from_z(z, z < depth - 1, z > 0, begin)
    hide_item(0)
    for load in loads[2 + LOADS :]:
        load.wait()
    for head in range(heads):
        cols = pl.ds(head * HD, HD)
        scale = jnp.broadcast_to(scales_ref[head : head + 1, :], (HD, scales_ref.shape[1])).T
        weights_ref[:, cols] = (quant_ref[:, cols].astype(jnp.float32) * scale).astype(jnp.bfloat16)
    for owner in order[2 * LINE :]:
        pick(owner)
    hide(beside).start()
    for step in range(1, group_total):
        weigh(step).start()
    weights[:, cols_of(part)] = weights_ref[slots_of(part), :]
    hidden[:, rows_of(here)] = picked[here]

    def send_piece(owner, act):
        source = outgoing.at[owner]
        index = 1 + lax.rem(here, per_chunk) * group_total + part
        mine = (owner == here) & (home == part)

        @pl.when(jnp.logical_not(mine))
        def _():
            act(remote(source, pieces_out.at[index], o_send.at[owner], o_recv.at[index], (owner, home)))

        if act is begin:

            @pl.when(mine)
            def _():
                pieces_out[index] = outgoing[owner]

    def produce(owner):
        with jax.named_scope("shared"):
            for row in range(2):
                share(owner, row, 1 - core).wait_recv()
        outgoing[owner] = lax.dot_general(
            weights[...], rotated[rows_of(owner), :], (((1,), (1,)), ((), ())),
            preferred_element_type=jnp.float32,
        ).astype(jnp.bfloat16)

    hidden_items = LINE * (depth - 1)
    sent = 1
    for stage in range(1, depth + 3):

        def take_z(sign, level):
            with jax.named_scope(f"z{stage}{sign}"):
                arrived(level * LINE + y, side)
            from_z(level, (sign < 0) & (z < depth - 1), (sign > 0) & (z > 0), begin)

        def take_x(sign, level):
            with jax.named_scope(f"x{stage}{sign}"):
                arrived(level * LINE + y, 1 - side)
            from_x(level, begin)

        def take_y(row):
            def act(sign, level):
                with jax.named_scope(f"y{stage}{sign}"):
                    arrived(level * LINE + 1 - y, row)
                from_y(level, row, begin)

            return act

        if stage < depth:
            at_levels(stage, take_z)
        at_levels(stage - 1, take_x)
        at_levels(stage - 1, take_y(side))
        at_levels(stage - 2, take_y(1 - side))
        for item in range(sent, min(sent + HIDE_EACH, hidden_items)):
            hide_item(item)
        sent = min(sent + HIDE_EACH, hidden_items)
        if stage == 1:
            with jax.named_scope("weigh"):
                for step in range(1, group_total):
                    weigh(step).wait_recv()
        at_levels(stage - 1, lambda sign, level: produce(level * LINE + y))
        at_levels(stage - 2, lambda sign, level: produce(level * LINE + 1 - y))
        at_levels(stage - 1, lambda sign, level: send_piece(level * LINE + y, begin))
        at_levels(stage - 2, lambda sign, level: send_piece(level * LINE + 1 - y, begin))

    with jax.named_scope("hidden"):
        for step in range(1, owners_n):
            hidden_from(lax.rem(here + step, owners_n)).wait_recv()

    def send_grad(step):
        target = lax.rem(part + step, group_total)
        return remote(
            grad_send.at[target], grad_out.at[part], g_send.at[step - 1], g_recv.at[step - 1], (here, target)
        )

    def reduce(step, carry):
        target = lax.rem(part + step, group_total)
        grad_send[target] = jnp.dot(
            hidden[...], rotated[:, cols_of(target)], preferred_element_type=jnp.float32
        ).astype(jnp.bfloat16)

        @pl.when(step > 1)
        def _():
            send_grad(step - 1).start()

        return carry

    with jax.named_scope("reduce"):
        lax.fori_loop(1, group_total + 1, reduce, 0)
    grad_out[part] = grad_send[part]

    mine_index = jnp.where(home == part, 1 + lax.rem(here, per_chunk) * group_total + part, 0)

    def landed(index):
        return remote(
            outgoing.at[0], pieces_out.at[index], o_send.at[0], o_recv.at[index], (here, partner)
        )

    def pass_on(index, to_chunk, slot, send):
        return remote(pieces_out.at[index], pieces_out.at[slot], e_send.at[send], o_recv.at[slot], (here, to_chunk))

    for index in (last_piece - 1, 1):

        @pl.when(mine_index != index)
        def _():
            with jax.named_scope("edge"):
                landed(index).wait_recv()

    @pl.when(part < group_total - 1)
    def _():
        pass_on(last_piece - 1, part + 1, 0, 0).start()

    @pl.when(part > 0)
    def _():
        pass_on(1, part - 1, last_piece, 1).start()

    for index in range(2, last_piece - 1):

        @pl.when(mine_index != index)
        def _():
            with jax.named_scope("landed"):
                landed(index).wait_recv()

    @pl.when(part < group_total - 1)
    def _():
        pass_on(last_piece - 1, part + 1, 0, 0).wait_send()
        landed(last_piece).wait_recv()

    @pl.when(part > 0)
    def _():
        pass_on(1, part - 1, last_piece, 1).wait_send()
        landed(0).wait_recv()

    with jax.named_scope("grads"):
        for step in range(1, group_total):
            send_grad(step).wait_send()
            remote(grad_send.at[0], grad_out.at[0], g_send.at[step - 1], g_recv.at[step - 1], (here, partner)).wait_recv()
    for owner in range(owners_n):
        send_piece(jnp.int32(owner), finish)
    for step in range(1, group_total):
        weigh(step).wait_send()
    for step in range(1, owners_n):
        hide(lax.rem(here + step, owners_n)).wait_send()
    from_z(z, z < depth - 1, z > 0, finish)
    for away in range(depth):
        if away:
            at_levels(
                away,
                lambda sign, level: from_z(level, (sign < 0) & (z < depth - 1), (sign > 0) & (z > 0), finish),
            )
        at_levels(away, lambda sign, level: from_x(level, finish))
        for row in range(2):
            at_levels(away, lambda sign, level, row=row: from_y(level, row, finish))


def exchange_plan(hidden_in, key_grad, positions, key_quant, key_scales, block_counts):
    owners_n = lax.axis_size("fsdp")
    group_total = lax.axis_size("tp")
    slot_count, width = key_quant.shape
    tokens_here, row_total = hidden_in.shape
    heads = key_scales.shape[1]
    quarter = slot_count // group_total
    chunk = row_total // group_total
    per_chunk = owners_n // group_total
    columns = width * group_total
    vmem = pl.BlockSpec(memory_space=pltpu.VMEM)
    anywhere = pl.BlockSpec(memory_space=pl.ANY)
    smem = pl.BlockSpec(memory_space=pltpu.SMEM)
    pieces_n = 2 + per_chunk * group_total
    dma = pltpu.SemaphoreType.DMA
    weight_grad, pieces = pl.pallas_call(
        functools.partial(exchange_kernel, owners_n, group_total),
        out_shape=(
            jax.ShapeDtypeStruct((group_total, quarter, width), jnp.bfloat16),
            jax.ShapeDtypeStruct((pieces_n, quarter, tokens_here), jnp.bfloat16),
        ),
        in_specs=[smem] + [anywhere] * 5,
        out_specs=(vmem,) * 2,
        scratch_shapes=[
            pltpu.VMEM((tokens_here, row_total), jnp.bfloat16),
            pltpu.VMEM((tokens_here, width), jnp.bfloat16),
            pltpu.VMEM((1, tokens_here), jnp.int32),
            pltpu.VMEM((slot_count, width), jnp.bfloat16),
            pltpu.VMEM((heads, slot_count), jnp.float32),
            pltpu.VMEM((slot_count, width), jnp.bfloat16),
            pltpu.VMEM((owners_n * tokens_here, columns), jnp.bfloat16),
            pltpu.VMEM((quarter, columns), jnp.bfloat16),
            pltpu.VMEM((owners_n, quarter, tokens_here), jnp.bfloat16),
            pltpu.VMEM((quarter, owners_n * tokens_here), jnp.bfloat16),
            pltpu.VMEM((owners_n, quarter, tokens_here), jnp.bfloat16),
            pltpu.VMEM((group_total, quarter, width), jnp.bfloat16),
            dma((4 + LOADS,)),
            dma((group_total - 1,)), dma((group_total - 1,)),
            dma((owners_n,)), dma((owners_n,)),
            dma((owners_n,)), dma((owners_n,)), dma((owners_n,)), dma((2 * owners_n,)), dma((2 * owners_n,)),
            dma((2 * owners_n,)), dma((2 * owners_n,)),
            dma((owners_n,)), dma((2,)), dma((pieces_n,)),
            dma((group_total - 1,)), dma((group_total - 1,)),
        ],
        compiler_params=pltpu.CompilerParams(has_side_effects=True, collective_id=0),
        name="exchange",
    )(block_counts, hidden_in, key_grad, positions.reshape(1, -1), key_quant, key_scales.T)

    margin = max(
        max(
            chunk * (owner // per_chunk) - offset_range(owner - 1, owners_n, row_total, slot_count)[0]
            for owner in range(per_chunk, owners_n, per_chunk)
        ),
        2 * quarter,
    ) if group_total > 1 else 2 * quarter
    pad = -(-(margin + slot_count) // 8) * 8
    return pl.pallas_call(
        functools.partial(assemble_kernel, owners_n, group_total, pad),
        out_shape=(
            jax.ShapeDtypeStruct((slot_count, width), jnp.bfloat16),
            jax.ShapeDtypeStruct((tokens_here, chunk), jnp.bfloat16),
        ),
        in_specs=[smem, vmem, vmem],
        out_specs=(vmem,) * 2,
        scratch_shapes=[pltpu.VMEM((chunk + 2 * pad, tokens_here), jnp.float32)],
        name="assemble",
    )(block_counts, pieces, weight_grad)


def rotary_backward(key_grad, positions):
    tokens_here = key_grad.shape[0]
    half_dim = HD // 2
    cotangent = key_grad.astype(jnp.float32).reshape(tokens_here, -1, HD)
    freq_idx = jnp.arange(half_dim, dtype=jnp.float32)
    inverse = jnp.exp(-(2.0 * freq_idx / HD) * math.log(rope_base))
    angles = positions.astype(jnp.float32)[:, None] * inverse[None, :]
    cosine = jnp.cos(angles)[:, None, :]
    sine_part = jnp.sin(angles)[:, None, :]
    lower_half = cotangent[..., :half_dim]
    upper_half = cotangent[..., half_dim:]
    back_lower = lower_half * cosine + upper_half * sine_part
    back_upper = upper_half * cosine - lower_half * sine_part
    joined = jnp.concatenate([back_lower, back_upper], axis=-1)
    return joined.reshape(tokens_here, -1).astype(jnp.bfloat16)


def slot_tables(block_counts, slot_count, row_total):
    offsets = jnp.cumsum(block_counts) - block_counts
    owners_n = block_counts.shape[0]
    slot_ids = jnp.arange(owners_n * slot_count, dtype=jnp.int32)
    within = slot_ids % slot_count
    live_counts = jnp.broadcast_to(block_counts[:, None], (owners_n, slot_count)).reshape(-1)
    base_rows = jnp.broadcast_to(offsets[:, None], (owners_n, slot_count)).reshape(-1)
    is_live = within < live_counts
    row_of_slot = jnp.where(is_live, base_rows + within, 0)
    row_ids = jnp.arange(row_total, dtype=jnp.int32)
    at_or_after = row_ids[:, None] >= offsets[None, :]
    owner_of_row = jnp.sum(at_or_after.astype(jnp.int32), axis=1) - 1
    row_begin = jnp.max(jnp.where(at_or_after, offsets[None, :], 0), axis=1)
    slot_of_row = owner_of_row * slot_count + row_ids - row_begin
    return (row_of_slot, is_live, slot_of_row)


def gather_plan(hidden_in, key_grad, positions, key_quant, key_scales, block_counts):
    slot_count = key_quant.shape[0]
    local_heads = key_scales.shape[1]
    row_total = hidden_in.shape[1]
    row_of_slot, is_live, slot_of_row = slot_tables(block_counts, slot_count, row_total)
    scaled = (
        key_quant.astype(jnp.float32).reshape(slot_count, local_heads, HD) * key_scales[:, :, None]
    )
    local_weights = scaled.astype(jnp.bfloat16).reshape(slot_count, local_heads * HD)
    rotated = rotary_backward(key_grad, positions)
    picked = jnp.where(
        is_live[None, :], jnp.take(hidden_in, row_of_slot, axis=1), jnp.zeros((), jnp.bfloat16)
    )
    weight_grad = lax.psum_scatter(
        lax.dot_general(
            picked, rotated, (((0,), (0,)), ((), ())), preferred_element_type=jnp.float32
        ),
        "fsdp",
        scatter_dimension=0,
        tiled=True,
    ).astype(jnp.bfloat16)
    group_total = lax.axis_size("tp")
    whole_slots = lax.all_gather(local_weights, "fsdp", axis=0, tiled=True)
    ordered = jnp.take(whole_slots, slot_of_row, axis=0)
    own_rows = lax.all_to_all(ordered, "tp", split_axis=0, concat_axis=1, tiled=True)
    all_heads = lax.all_gather(rotated, "tp", axis=1, tiled=True)
    tokens_here = all_heads.shape[0]
    feature_here = own_rows.shape[0]
    heads_grouped = all_heads.reshape(tokens_here, group_total, -1)
    rows_grouped = own_rows.reshape(feature_here, group_total, -1)
    group_part = jnp.einsum(
        "tgk,dgk->gtd", heads_grouped, rows_grouped, preferred_element_type=jnp.float32
    ).astype(jnp.bfloat16)
    input_grad = jnp.sum(group_part.astype(jnp.float32), axis=0).astype(jnp.bfloat16)
    return (weight_grad, input_grad)


def per_device(hidden_in, key_grad, positions, key_quant, key_scales, block_counts):
    tokens_here, row_total = hidden_in.shape
    slot_count, width = key_quant.shape
    fits = exchange_fits(
        lax.axis_size("fsdp"), lax.axis_size("tp"), slot_count, row_total, tokens_here, width
    )
    plan = exchange_plan if fits else gather_plan
    return plan(hidden_in, key_grad, positions, key_quant, key_scales, block_counts)


def solution(mesh):
    in_specs = (P("fsdp", None), P("fsdp", "tp"), P("fsdp"), P("fsdp", "tp"), P("fsdp", "tp"), P())
    out_specs = (P("fsdp", "tp"), P("fsdp", "tp"))
    return jax.shard_map(
        per_device, mesh=mesh, in_specs=in_specs, out_specs=out_specs, check_vma=False
    )
```

time: 63.4 us -> 50.1 us (0.79)
  Pallas kernels: 60.7 us -> 49.3 us
  other arithmetic: 1.62 us -> 0 us
    pallas_call x1, Pallas kernels: 54.7 us -> 46.7 us  [exchange_plan(): pl.pallas_call(functools.partial(exchange_kernel, owners_n, group_total),...]
    pallas_call x1 -> x0, Pallas kernels: 3.43 us -> none  [exchange_plan(): pl.pallas_call(functools.partial(pick_kernel, owners_n, group_total, span...]
    sin x1 -> x0, other arithmetic: 0.95 us -> none  [rotary_tables(): return (jnp.cos(angles), jnp.sin(angles))]
    convert_element_type x1 -> x0, other arithmetic: 0.66 us -> none  [rotary_tables(): angles = positions.astype(jnp.float32)[:, None] * inverse[None, :]]
where the time goes in v1:
time: 50.1 us; the launch traced here: 49.9 us
  Pallas kernels  49.3 us (98%)
  between operations  0.64 us (1%)
    pallas_call x1, Pallas kernels, exchange_plan(): pl.pallas_call(functools.partial(exchange_kernel, owners_n, group_total),...  46.7 us
    pallas_call x1, Pallas kernels, exchange_plan(): pl.pallas_call(functools.partial(assemble_kernel, owners_n, group_total,...  2.54 us

profile of v1, /device:TPU:1, one launch (start us, length us, event | category | flops | bytes accessed | tf_op | source)
XLA Modules:
  0.0 49.9 jit_solution(16017289704272747663)
XLA Ops:
  0.6 46.7 %exchange.1 = (bf16[4,272,256]{2,1,0:T(8,128)(2,1)}, bf16[10,272,128]{2,1,0:T(8,128)(2,1)}) custom-call(s32[8]{0:T(128)} %counts_ref.3, bf16[128,8192]{1,0:T(8,128)(2,1)} %hidden_any.1, bf16[128,256]{1,0:T(8,128)(2,1)} %grad_any.1, s32[1,128]{1,0:T(1,128)} %bitcast.3, bf16[1088,256]{1,0:T(8,128)(2,1)} %quant_any.1, f32[2,1088]{1,0:T(2,128)} %bitcast.2), custom_call_target="tpu_custom_call" | custom-call | tf_op jit(solution)/shard_map/exchange/pallas_call | solution.py:476
  47.4 2.5 %assemble.1 = (bf16[1088,256]{1,0:T(8,128)(2,1)}, bf16[128,2048]{1,0:T(8,128)(2,1)}) custom-call(s32[8]{0:T(128)} %counts_ref.3, bf16[10,272,128]{2,1,0:T(8,128)(2,1)} %get-tuple-element.4.pieces_ref, bf16[4,272,256]{2,1,0:T(8,128)(2,1)} %get-tuple-element.5.grad_ref), custom_call_target="tpu_custom_call" | custom-call | tf_op jit(solution)/shard_map/assemble/pallas_call | solution.py:517

commit v2 on v1

--- a/solution.py
+++ b/solution.py
@@ -12,7 +12,10 @@
 LANES = 128
 LINE = 2
 LOADS = 4
-HIDE_EACH = 2
+VMEM_LIMIT = 24 * 2**20
+WEIGH_AT = 4
+WEIGH_NEXT = 1
+OUT_AT = 4
 MESH = pl.DeviceIdType.MESH
 
 rope_base = 500000.0
@@ -101,8 +104,9 @@
     hidden_in, grad_ref, positions_ref, quant_ref, scales_ref,
     weights_ref, rotated, weights, picked, hidden, outgoing, grad_send,
     load_sem, w_send, w_recv, h_send, h_recv,
-    up_send, down_send, x_send, y_send, net_recv, pair_send, pair_recv,
+    z_send, first_send, second_send, net_recv, pair_send, pair_recv,
     o_send, e_send, o_recv, g_send, g_recv,
+    column_in, beside_in,
 ):
     here = lax.axis_index("fsdp")
     part = lax.axis_index("tp")
@@ -134,11 +138,23 @@
     for load in loads:
         load.start()
     barrier = pltpu.get_barrier_semaphore()
-    for step in range(owners_n):
+
+    def greet(where):
+        pl.semaphore_signal(barrier, inc=1, device_id=where, device_id_type=MESH)
+
+    @pl.when(z > 0)
+    def _():
+        greet((here - LINE, part))
+
+    @pl.when(z < depth - 1)
+    def _():
+        greet((here + LINE, part))
+
+    for row in range(LINE):
         for turn in range(group_total):
-            if step or turn:
-                where = (lax.rem(here + step, owners_n), lax.rem(part + turn, group_total))
-                pl.semaphore_signal(barrier, inc=1, device_id=where, device_id_type=MESH)
+            if row or turn:
+                greet((z * LINE + lax.rem(y + row, LINE), lax.rem(part + turn, group_total)))
+    near_n = LINE * group_total - 1 + jnp.where(z > 0, 1, 0) + jnp.where(z < depth - 1, 1, 0)
 
     def remote(src, dst, send, recv, where):
         return pltpu.make_async_remote_copy(
@@ -154,11 +170,12 @@
     def slots_of(group):
         return pl.ds(pl.multiple_of(group * quarter, 16), quarter)
 
-    def weigh(step):
-        target = lax.rem(part + step, group_total)
+    peers = (lax.rem(partner + 2, group_total), across, partner)
+
+    def weigh(kind):
         return remote(
-            weights_ref.at[slots_of(target), :], weights.at[:, cols_of(part)],
-            w_send.at[step - 1], w_recv.at[step - 1], (here, target),
+            weights_ref.at[slots_of(peers[kind]), :], weights.at[:, cols_of(part)],
+            w_send.at[kind], w_recv.at[kind], (here, peers[kind]),
         )
 
     def hide(target):
@@ -222,16 +239,8 @@
         swapped = jnp.concatenate([values[:, HD // 2 :], values[:, : HD // 2]], axis=1)
         cols = pl.ds(pl.multiple_of(part * width + head * HD, HD), HD)
         rotated[rows_of(here), cols] = (values * cosine + swapped * sine).astype(jnp.bfloat16)
-    for load in loads[2 : 2 + LOADS]:
-        load.wait()
-    order = []
-    for low in range((depth + 1) // 2):
-        for level in dict.fromkeys((depth - 1 - low, low)):
-            order += [level * LINE + row for row in range(LINE)]
-    for owner in order[: 2 * LINE]:
-        pick(owner)
     with jax.named_scope("barrier"):
-        pl.semaphore_wait(barrier, owners_n * group_total - 1)
+        pl.semaphore_wait(barrier, near_n)
 
     def begin(copy):
         copy.start()
@@ -239,31 +248,43 @@
     def finish(copy):
         copy.wait_send()
 
-    def from_z(level, up, down, act):
-        owner = level * LINE + y
-
-        @pl.when(up)
-        def _():
-            act(relay(owner, side, up_send.at[owner], (here + LINE, part)))
-
-        @pl.when(down)
-        def _():
-            act(relay(owner, side, down_send.at[owner], (here - LINE, part)))
-
-        act(relay(owner, side, x_send.at[owner], (here, across)))
-        act(relay(owner, side, y_send.at[owner * 2 + side], (beside, part)))
-        act(share(owner, side, core))
-
-    def from_x(level, act):
-        owner = level * LINE + y
-        act(relay(owner, 1 - side, y_send.at[owner * 2 + 1 - side], (beside, part)))
-        act(share(owner, 1 - side, core))
-
-    def from_y(level, row, act):
-        act(share(level * LINE + 1 - y, row, core))
+    def own_row(level):
+        return level * LINE + y, side
+
+    def first_row(level):
+        return level * LINE + jnp.where(core == 0, y, 1 - y), jnp.where(core == 0, 1 - side, side)
+
+    def second_row(level):
+        return level * LINE + jnp.where(core == 0, 1 - y, y), jnp.where(core == 0, side, 1 - side)
+
+    def last_row(level):
+        return level * LINE + 1 - y, 1 - side
+
+    first_to = (jnp.where(core == 0, here, beside), jnp.where(core == 0, across, part))
+    second_to = (jnp.where(core == 0, beside, here), jnp.where(core == 0, part, across))
+
+    def climb(level):
+        return relay(*own_row(z), z_send.at[level], (level * LINE + y, part))
+
+    def from_z(level, act):
+        owner, row = own_row(level)
+        act(relay(owner, row, first_send.at[owner], first_to))
+        act(relay(owner, row, second_send.at[owner * 2 + row], second_to))
+        act(share(owner, row, core))
+
+    def from_first(level, act):
+        owner, row = first_row(level)
+        act(relay(owner, row, second_send.at[owner * 2 + row], second_to))
+        act(share(owner, row, core))
+
+    def from_second(level, act):
+        act(share(*second_row(level), core))
+
+    def from_last(level, act):
+        act(share(*last_row(level), core))
 
     def arrived(owner, row):
-        relay(owner, row, x_send.at[0], (here, across)).wait_recv()
+        relay(owner, row, first_send.at[0], first_to).wait_recv()
 
     def levels(away):
         for sign in (-1, 1) if away else (1,):
@@ -277,33 +298,47 @@
                 def _():
                     act(sign, level)
 
-    def hide_item(item):
-        level, row = item // LINE, (1 - y if item % LINE == 0 else y)
-        above = depth - 1 - level
-
-        @pl.when(above > z)
+    def tell(level, known):
+        pl.semaphore_signal(
+            column_in.at[known], inc=1, device_id=(level * LINE + y, part), device_id_type=MESH
+        )
+
+    def heard(sign, known):
+        @pl.when((z - sign >= 0) & (z - sign < depth))
         def _():
-            hide(above * LINE + row).start()
-
-        @pl.when(level < z)
-        def _():
-            hide(level * LINE + row).start()
-
-    from_z(z, z < depth - 1, z > 0, begin)
-    hide_item(0)
+            tell(z - sign, known)
+
+    at_levels(1, heard)
+    at_levels(1, lambda sign, level: climb(level).start())
+    from_z(z, begin)
+
+    def farther(sign, level):
+        pl.semaphore_wait(column_in.at[level], 1)
+        heard(sign, level)
+        climb(level).start()
+
+    for away in range(2, depth):
+        at_levels(away, farther)
+    pl.semaphore_signal(beside_in, inc=1, device_id=(beside, part), device_id_type=MESH)
+    for load in loads[2 : 2 + LOADS]:
+        load.wait()
+    for owner in range(owners_n):
+        pick(owner)
     for load in loads[2 + LOADS :]:
         load.wait()
     for head in range(heads):
         cols = pl.ds(head * HD, HD)
         scale = jnp.broadcast_to(scales_ref[head : head + 1, :], (HD, scales_ref.shape[1])).T
         weights_ref[:, cols] = (quant_ref[:, cols].astype(jnp.float32) * scale).astype(jnp.bfloat16)
-    for owner in order[2 * LINE :]:
-        pick(owner)
-    hide(beside).start()
-    for step in range(1, group_total):
-        weigh(step).start()
     weights[:, cols_of(part)] = weights_ref[slots_of(part), :]
     hidden[:, rows_of(here)] = picked[here]
+    weigh(1).start()
+    weigh(2).start()
+    pl.semaphore_wait(beside_in, 1)
+    for row in (1 - y, y):
+        for away in range(1, depth):
+            at_levels(away, lambda sign, level, row=row: hide(level * LINE + row).start())
+    hide(beside).start()
 
     def send_piece(owner, act):
         source = outgoing.at[owner]
@@ -329,70 +364,69 @@
             preferred_element_type=jnp.float32,
         ).astype(jnp.bfloat16)
 
-    hidden_items = LINE * (depth - 1)
-    sent = 1
+    ready, made = [], []
     for stage in range(1, depth + 3):
 
-        def take_z(sign, level):
-            with jax.named_scope(f"z{stage}{sign}"):
-                arrived(level * LINE + y, side)
-            from_z(level, (sign < 0) & (z < depth - 1), (sign > 0) & (z > 0), begin)
-
-        def take_x(sign, level):
-            with jax.named_scope(f"x{stage}{sign}"):
-                arrived(level * LINE + y, 1 - side)
-            from_x(level, begin)
-
-        def take_y(row):
+        def take(name, row_of, pass_on):
             def act(sign, level):
-                with jax.named_scope(f"y{stage}{sign}"):
-                    arrived(level * LINE + 1 - y, row)
-                from_y(level, row, begin)
+                with jax.named_scope(f"{name}{stage}{sign}"):
+                    arrived(*row_of(level))
+                pass_on(sign, level)
 
             return act
 
         if stage < depth:
-            at_levels(stage, take_z)
-        at_levels(stage - 1, take_x)
-        at_levels(stage - 1, take_y(side))
-        at_levels(stage - 2, take_y(1 - side))
-        for item in range(sent, min(sent + HIDE_EACH, hidden_items)):
-            hide_item(item)
-        sent = min(sent + HIDE_EACH, hidden_items)
-        if stage == 1:
+            at_levels(stage, take("z", own_row, lambda sign, level: from_z(level, begin)))
+        at_levels(stage - 1, take("first", first_row, lambda sign, level: from_first(level, begin)))
+        at_levels(stage - 1, take("second", second_row, lambda sign, level: from_second(level, begin)))
+        at_levels(stage - 2, take("last", last_row, lambda sign, level: from_last(level, begin)))
+        if stage == WEIGH_NEXT:
+            weigh(0).start()
+        if stage == WEIGH_AT:
             with jax.named_scope("weigh"):
-                for step in range(1, group_total):
-                    weigh(step).wait_recv()
-        at_levels(stage - 1, lambda sign, level: produce(level * LINE + y))
-        at_levels(stage - 2, lambda sign, level: produce(level * LINE + 1 - y))
-        at_levels(stage - 1, lambda sign, level: send_piece(level * LINE + y, begin))
-        at_levels(stage - 2, lambda sign, level: send_piece(level * LINE + 1 - y, begin))
+                for kind in range(3):
+                    weigh(kind).wait_recv()
+        ready.append((stage - 1, y))
+        ready.append((stage - 2, 1 - y))
+        if stage >= WEIGH_AT:
+            for away, row in ready:
+                at_levels(away, lambda sign, level, row=row: produce(level * LINE + row))
+            made += ready
+            ready = []
+        if stage >= OUT_AT:
+            for away, row in made[::-1]:
+                at_levels(away, lambda sign, level, row=row: send_piece(level * LINE + row, begin))
+            made = []
 
     with jax.named_scope("hidden"):
         for step in range(1, owners_n):
             hidden_from(lax.rem(here + step, owners_n)).wait_recv()
 
-    def send_grad(step):
-        target = lax.rem(part + step, group_total)
+    def send_grad(kind):
         return remote(
-            grad_send.at[target], grad_out.at[part], g_send.at[step - 1], g_recv.at[step - 1], (here, target)
-        )
-
-    def reduce(step, carry):
-        target = lax.rem(part + step, group_total)
-        grad_send[target] = jnp.dot(
-            hidden[...], rotated[:, cols_of(target)], preferred_element_type=jnp.float32
-        ).astype(jnp.bfloat16)
-
-        @pl.when(step > 1)
-        def _():
-            send_grad(step - 1).start()
-
-        return carry
+            grad_send.at[peers[kind]], grad_out.at[part], g_send.at[kind], g_recv.at[kind], (here, peers[kind])
+        )
 
     with jax.named_scope("reduce"):
-        lax.fori_loop(1, group_total + 1, reduce, 0)
+        for kind, target in enumerate(peers + (part,)):
+            grad_send[target] = jnp.dot(
+                hidden[...], rotated[:, cols_of(target)], preferred_element_type=jnp.float32
+            ).astype(jnp.bfloat16)
+            if kind:
+                send_grad(kind - 1).start()
     grad_out[part] = grad_send[part]
+
+    for kind in range(3):
+        weigh(kind).wait_send()
+    for step in range(1, owners_n):
+        hide(lax.rem(here + step, owners_n)).wait_send()
+    for away in range(depth):
+        if away:
+            at_levels(away, lambda sign, level: climb(level).wait_send())
+        at_levels(away, lambda sign, level: from_z(level, finish))
+        at_levels(away, lambda sign, level: from_first(level, finish))
+        at_levels(away, lambda sign, level: from_second(level, finish))
+        at_levels(away, lambda sign, level: from_last(level, finish))
 
     mine_index = jnp.where(home == part, 1 + lax.rem(here, per_chunk) * group_total + part, 0)
 
@@ -436,26 +470,12 @@
         pass_on(1, part - 1, last_piece, 1).wait_send()
         landed(0).wait_recv()
 
-    with jax.named_scope("grads"):
-        for step in range(1, group_total):
-            send_grad(step).wait_send()
-            remote(grad_send.at[0], grad_out.at[0], g_send.at[step - 1], g_recv.at[step - 1], (here, partner)).wait_recv()
     for owner in range(owners_n):
         send_piece(jnp.int32(owner), finish)
-    for step in range(1, group_total):
-        weigh(step).wait_send()
-    for step in range(1, owners_n):
-        hide(lax.rem(here + step, owners_n)).wait_send()
-    from_z(z, z < depth - 1, z > 0, finish)
-    for away in range(depth):
-        if away:
-            at_levels(
-                away,
-                lambda sign, level: from_z(level, (sign < 0) & (z < depth - 1), (sign > 0) & (z > 0), finish),
-            )
-        at_levels(away, lambda sign, level: from_x(level, finish))
-        for row in range(2):
-            at_levels(away, lambda sign, level, row=row: from_y(level, row, finish))
+    with jax.named_scope("grads"):
+        for kind in range(3):
+            send_grad(kind).wait_send()
+            remote(grad_send.at[0], grad_out.at[0], g_send.at[kind], g_recv.at[kind], (here, partner)).wait_recv()
 
 
 def exchange_plan(hidden_in, key_grad, positions, key_quant, key_scales, block_counts):
@@ -469,7 +489,7 @@
     per_chunk = owners_n // group_total
     columns = width * group_total
     vmem = pl.BlockSpec(memory_space=pltpu.VMEM)
-    anywhere = pl.BlockSpec(memory_space=pl.ANY)
+    anywhere = pl.BlockSpec(memory_space=pltpu.HBM)
     smem = pl.BlockSpec(memory_space=pltpu.SMEM)
     pieces_n = 2 + per_chunk * group_total
     dma = pltpu.SemaphoreType.DMA
@@ -497,14 +517,20 @@
             dma((4 + LOADS,)),
             dma((group_total - 1,)), dma((group_total - 1,)),
             dma((owners_n,)), dma((owners_n,)),
-            dma((owners_n,)), dma((owners_n,)), dma((owners_n,)), dma((2 * owners_n,)), dma((2 * owners_n,)),
+            dma((owners_n // LINE,)), dma((owners_n,)), dma((2 * owners_n,)), dma((2 * owners_n,)),
             dma((2 * owners_n,)), dma((2 * owners_n,)),
             dma((owners_n,)), dma((2,)), dma((pieces_n,)),
             dma((group_total - 1,)), dma((group_total - 1,)),
+            pltpu.SemaphoreType.REGULAR((owners_n // LINE,)), pltpu.SemaphoreType.REGULAR,
         ],
-        compiler_params=pltpu.CompilerParams(has_side_effects=True, collective_id=0),
+        compiler_params=pltpu.CompilerParams(
+            has_side_effects=True, collective_id=0, vmem_limit_bytes=VMEM_LIMIT
+        ),
         name="exchange",
-    )(block_counts, hidden_in, key_grad, positions.reshape(1, -1), key_quant, key_scales.T)
+    )(*(
+        pltpu.with_memory_space_constraint(array, pltpu.HBM)
+        for array in (block_counts, hidden_in, key_grad, positions.reshape(1, -1), key_quant, key_scales.T)
+    ))
 
     margin = max(
         max(
@@ -523,8 +549,9 @@
         in_specs=[smem, vmem, vmem],
         out_specs=(vmem,) * 2,
         scratch_shapes=[pltpu.VMEM((chunk + 2 * pad, tokens_here), jnp.float32)],
+        compiler_params=pltpu.CompilerParams(vmem_limit_bytes=VMEM_LIMIT),
         name="assemble",
-    )(block_counts, pieces, weight_grad)
+    )(pltpu.with_memory_space_constraint(block_counts, pltpu.HBM), pieces, weight_grad)
 
 
 def rotary_backward(key_grad, positions):

time: 50.1 us -> 45.6 us (0.910)
  Pallas kernels: 49.3 us -> 44.8 us
    pallas_call x1, Pallas kernels: 46.7 us -> 42.9 us  [exchange_plan(): pl.pallas_call(functools.partial(exchange_kernel, owners_n, group_total),...]
    pallas_call x1, Pallas kernels: 2.54 us -> 1.94 us  [exchange_plan(): pl.pallas_call(functools.partial(assemble_kernel, owners_n, group_total,...]
where the time goes in v2:
time: 45.6 us; the launch traced here: 45.5 us
  Pallas kernels  44.8 us (98%)
  between operations  0.64 us (1%)
    pallas_call x1, Pallas kernels, exchange_plan(): pl.pallas_call(functools.partial(exchange_kernel, owners_n, group_total),...  42.9 us
    pallas_call x1, Pallas kernels, exchange_plan(): pl.pallas_call(functools.partial(assemble_kernel, owners_n, group_total,...  1.94 us

profile of v2, /device:TPU:1, one launch (start us, length us, event | category | flops | bytes accessed | tf_op | source)
XLA Modules:
  0.0 45.5 jit_solution(17225249234505637594)
XLA Ops:
  0.6 42.9 %exchange.1 = (bf16[4,272,256]{2,1,0:T(8,128)(2,1)S(1)}, bf16[10,272,128]{2,1,0:T(8,128)(2,1)S(1)}) custom-call(s32[8]{0:T(128)} %counts_ref.3, bf16[128,8192]{1,0:T(8,128)(2,1)} %hidden_any.1, bf16[128,256]{1,0:T(8,128)(2,1)} %grad_any.1, s32[1,128]{1,0:T(1,128)} %bitcast.3, bf16[1088,256]{1,0:T(8,128)(2,1)} %quant_any.1, f32[2,1088]{1,0:T(2,128)} %bitcast.2), custom_call_target="tpu_custom_call" | custom-call | tf_op jit(solution)/shard_map/exchange/pallas_call | solution.py:496
  43.5 1.9 %assemble.1 = (bf16[1088,256]{1,0:T(8,128)(2,1)}, bf16[128,2048]{1,0:T(8,128)(2,1)}) custom-call(s32[8]{0:T(128)} %counts_ref.3, bf16[10,272,128]{2,1,0:T(8,128)(2,1)S(1)} %get-tuple-element.4.pieces_ref, bf16[4,272,256]{2,1,0:T(8,128)(2,1)S(1)} %get-tuple-element.5.grad_ref), custom_call_target="tpu_custom_call" | custom-call | tf_op jit(solution)/shard_map/assemble/pallas_call | solution.py:543

commit v3 on v2

--- a/solution.py
+++ b/solution.py
@@ -12,10 +12,14 @@
 LANES = 128
 LINE = 2
 LOADS = 4
+WRITES = 4
 VMEM_LIMIT = 24 * 2**20
+SIDE_CORE = 1
+HIDE_AT = (1, 3)
+WEIGH_FROM = (2, 1)
 WEIGH_AT = 4
-WEIGH_NEXT = 1
-OUT_AT = 4
+OUT_AT = 5
+EARLY = 0
 MESH = pl.DeviceIdType.MESH
 
 rope_base = 500000.0
@@ -32,7 +36,7 @@
 def exchange_fits(owners_n, group_total, slot_count, row_total, tokens_here, width):
     if group_total != 2 * LINE or owners_n % group_total or owners_n % LINE or slot_count % (16 * group_total):
         return False
-    if tokens_here % LANES or width % LANES or row_total % group_total or (row_total // group_total) % LANES:
+    if tokens_here % LANES or width % LANES or row_total % group_total or (row_total // group_total) % (WRITES * LANES):
         return False
     quarter = slot_count // group_total
     chunk = row_total // group_total
@@ -59,10 +63,18 @@
     return True
 
 
-def assemble_kernel(owners_n, group_total, pad, counts_ref, pieces_ref, grad_ref, grad_out, out_ref, rows):
+def assemble_kernel(
+    owners_n, group_total, pad, counts_ref, pieces_ref, grad_ref, grad_out, input_out, rows, out_ref, sems
+):
     chunk_at = lax.axis_index("tp")
     chunk = out_ref.shape[1]
     quarter = pieces_ref.shape[1]
+    copies = []
+    for part in range(group_total):
+        copies.append(
+            pltpu.make_async_copy(grad_ref.at[part], grad_out.at[pl.ds(part * quarter, quarter), :], sems.at[part])
+        )
+        copies[-1].start()
     per_chunk = owners_n // group_total
     offsets = []
     offset = jnp.int32(0)
@@ -81,8 +93,6 @@
     def place(index, begin):
         rows[pl.ds(jnp.clip(begin, 0, limit), quarter), :] = pieces_ref[index].astype(jnp.float32)
 
-    for part in range(group_total):
-        grad_out[pl.ds(part * quarter, quarter), :] = grad_ref[part]
     origin = pad - chunk_at * chunk
     first = chunk_at * per_chunk
     below = first_row(first - 1) + (group_total - 1) * quarter + origin
@@ -96,6 +106,12 @@
     place(last, jnp.where(chunk_at < group_total - 1, above, limit))
     for at in range(0, chunk, LANES):
         out_ref[:, pl.ds(at, LANES)] = rows[pl.ds(pad + at, LANES), :].T.astype(jnp.bfloat16)
+        if (at + LANES) % (chunk // WRITES) == 0:
+            done = pl.ds(at + LANES - chunk // WRITES, chunk // WRITES)
+            copies.append(pltpu.make_async_copy(out_ref.at[:, done], input_out.at[:, done], sems.at[len(copies)]))
+            copies[-1].start()
+    for copy in copies:
+        copy.wait()
 
 
 def exchange_kernel(
@@ -105,7 +121,7 @@
     weights_ref, rotated, weights, picked, hidden, outgoing, grad_send,
     load_sem, w_send, w_recv, h_send, h_recv,
     z_send, first_send, second_send, net_recv, pair_send, pair_recv,
-    o_send, e_send, o_recv, g_send, g_recv,
+    o_send, b_send, e_send, o_recv, g_send, g_recv,
     column_in, beside_in,
 ):
     here = lax.axis_index("fsdp")
@@ -251,17 +267,19 @@
     def own_row(level):
         return level * LINE + y, side
 
+    sideways = core == SIDE_CORE
+
     def first_row(level):
-        return level * LINE + jnp.where(core == 0, y, 1 - y), jnp.where(core == 0, 1 - side, side)
+        return level * LINE + jnp.where(sideways, y, 1 - y), jnp.where(sideways, 1 - side, side)
 
     def second_row(level):
-        return level * LINE + jnp.where(core == 0, 1 - y, y), jnp.where(core == 0, side, 1 - side)
+        return level * LINE + jnp.where(sideways, 1 - y, y), jnp.where(sideways, side, 1 - side)
 
     def last_row(level):
         return level * LINE + 1 - y, 1 - side
 
-    first_to = (jnp.where(core == 0, here, beside), jnp.where(core == 0, across, part))
-    second_to = (jnp.where(core == 0, beside, here), jnp.where(core == 0, part, across))
+    first_to = (jnp.where(sideways, here, beside), jnp.where(sideways, across, part))
+    second_to = (jnp.where(sideways, beside, here), jnp.where(sideways, part, across))
 
     def climb(level):
         return relay(*own_row(z), z_send.at[level], (level * LINE + y, part))
@@ -332,13 +350,31 @@
         weights_ref[:, cols] = (quant_ref[:, cols].astype(jnp.float32) * scale).astype(jnp.bfloat16)
     weights[:, cols_of(part)] = weights_ref[slots_of(part), :]
     hidden[:, rows_of(here)] = picked[here]
-    weigh(1).start()
     weigh(2).start()
-    pl.semaphore_wait(beside_in, 1)
-    for row in (1 - y, y):
-        for away in range(1, depth):
-            at_levels(away, lambda sign, level, row=row: hide(level * LINE + row).start())
-    hide(beside).start()
+    nearest = jnp.where(z > 0, z - 1, z + 1)
+    hide(nearest * LINE + y).start()
+
+    def hide_same(sign, level):
+        @pl.when(level != nearest)
+        def _():
+            hide(level * LINE + y).start()
+
+    def release(stage):
+        if stage == HIDE_AT[0]:
+            for away in range(1, depth):
+                at_levels(away, hide_same)
+        if stage == HIDE_AT[1]:
+            pl.semaphore_wait(beside_in, 1)
+            for away in range(1, depth):
+                at_levels(away, lambda sign, level: hide(level * LINE + 1 - y).start())
+            hide(beside).start()
+        for kind, at in enumerate(WEIGH_FROM):
+            if stage == at:
+                weigh(kind).start()
+
+    near = lax.rem(here, per_chunk)
+    after_mine = (near == per_chunk - 1) & (part == group_total - 1) & (home < group_total - 1) & (lax.rem(home, 2) == 1)
+    before_mine = (near == 0) & (part == 0) & (home > 0) & (lax.rem(home, 2) == 0)
 
     def send_piece(owner, act):
         source = outgoing.at[owner]
@@ -348,6 +384,14 @@
         @pl.when(jnp.logical_not(mine))
         def _():
             act(remote(source, pieces_out.at[index], o_send.at[owner], o_recv.at[index], (owner, home)))
+
+        @pl.when(after_mine)
+        def _():
+            act(remote(source, pieces_out.at[0], b_send.at[owner], o_recv.at[0], (owner, home + 1)))
+
+        @pl.when(before_mine)
+        def _():
+            act(remote(source, pieces_out.at[last_piece], b_send.at[owner], o_recv.at[last_piece], (owner, home - 1)))
 
         if act is begin:
 
@@ -380,18 +424,25 @@
         at_levels(stage - 1, take("first", first_row, lambda sign, level: from_first(level, begin)))
         at_levels(stage - 1, take("second", second_row, lambda sign, level: from_second(level, begin)))
         at_levels(stage - 2, take("last", last_row, lambda sign, level: from_last(level, begin)))
-        if stage == WEIGH_NEXT:
-            weigh(0).start()
+        release(stage)
         if stage == WEIGH_AT:
             with jax.named_scope("weigh"):
                 for kind in range(3):
                     weigh(kind).wait_recv()
         ready.append((stage - 1, y))
         ready.append((stage - 2, 1 - y))
+        ready = [(away, row) for away, row in ready if 0 <= away < depth]
         if stage >= WEIGH_AT:
+            due = None
             for away, row in ready:
                 at_levels(away, lambda sign, level, row=row: produce(level * LINE + row))
-            made += ready
+                if due:
+                    at_levels(due[0], lambda sign, level, row=due[1]: send_piece(level * LINE + row, begin))
+                due = (away, row) if away <= EARLY else None
+                if not due:
+                    made.append((away, row))
+            if due:
+                made.append(due)
             ready = []
         if stage >= OUT_AT:
             for away, row in made[::-1]:
@@ -445,13 +496,13 @@
             with jax.named_scope("edge"):
                 landed(index).wait_recv()
 
-    @pl.when(part < group_total - 1)
+    @pl.when(core == 0)
     def _():
-        pass_on(last_piece - 1, part + 1, 0, 0).start()
-
-    @pl.when(part > 0)
+        pass_on(last_piece - 1, partner, 0, 0).start()
+
+    @pl.when(core == 1)
     def _():
-        pass_on(1, part - 1, last_piece, 1).start()
+        pass_on(1, partner, last_piece, 1).start()
 
     for index in range(2, last_piece - 1):
 
@@ -460,15 +511,23 @@
             with jax.named_scope("landed"):
                 landed(index).wait_recv()
 
+    @pl.when(core == 0)
+    def _():
+        pass_on(last_piece - 1, partner, 0, 0).wait_send()
+
+    @pl.when(core == 1)
+    def _():
+        pass_on(1, partner, last_piece, 1).wait_send()
+
     @pl.when(part < group_total - 1)
     def _():
-        pass_on(last_piece - 1, part + 1, 0, 0).wait_send()
-        landed(last_piece).wait_recv()
+        with jax.named_scope("above"):
+            landed(last_piece).wait_recv()
 
     @pl.when(part > 0)
     def _():
-        pass_on(1, part - 1, last_piece, 1).wait_send()
-        landed(0).wait_recv()
+        with jax.named_scope("below"):
+            landed(0).wait_recv()
 
     for owner in range(owners_n):
         send_piece(jnp.int32(owner), finish)
@@ -519,7 +578,7 @@
             dma((owners_n,)), dma((owners_n,)),
             dma((owners_n // LINE,)), dma((owners_n,)), dma((2 * owners_n,)), dma((2 * owners_n,)),
             dma((2 * owners_n,)), dma((2 * owners_n,)),
-            dma((owners_n,)), dma((2,)), dma((pieces_n,)),
+            dma((owners_n,)), dma((owners_n,)), dma((2,)), dma((pieces_n,)),
             dma((group_total - 1,)), dma((group_total - 1,)),
             pltpu.SemaphoreType.REGULAR((owners_n // LINE,)), pltpu.SemaphoreType.REGULAR,
         ],
@@ -547,8 +606,12 @@
             jax.ShapeDtypeStruct((tokens_here, chunk), jnp.bfloat16),
         ),
         in_specs=[smem, vmem, vmem],
-        out_specs=(vmem,) * 2,
-        scratch_shapes=[pltpu.VMEM((chunk + 2 * pad, tokens_here), jnp.float32)],
+        out_specs=(anywhere,) * 2,
+        scratch_shapes=[
+            pltpu.VMEM((chunk + 2 * pad, tokens_here), jnp.float32),
+            pltpu.VMEM((tokens_here, chunk), jnp.bfloat16),
+            dma((group_total + WRITES,)),
+        ],
         compiler_params=pltpu.CompilerParams(vmem_limit_bytes=VMEM_LIMIT),
         name="assemble",
     )(pltpu.with_memory_space_constraint(block_counts, pltpu.HBM), pieces, weight_grad)

time: 45.6 us -> 44 us (0.965)
  Pallas kernels: 44.8 us -> 42.9 us
    pallas_call x1, Pallas kernels: 42.9 us -> 41.1 us  [exchange_plan(): pl.pallas_call(functools.partial(exchange_kernel, owners_n, group_total),...]
where the time goes in v3:
time: 44 us; the launch traced here: 43.5 us
  Pallas kernels  42.9 us (98%)
  between operations  0.64 us (1%)
    pallas_call x1, Pallas kernels, exchange_plan(): pl.pallas_call(functools.partial(exchange_kernel, owners_n, group_total),...  41.1 us
    pallas_call x1, Pallas kernels, exchange_plan(): pl.pallas_call(functools.partial(assemble_kernel, owners_n, group_total,...  1.77 us

profile of v3, /device:TPU:1, one launch (start us, length us, event | category | flops | bytes accessed | tf_op | source)
XLA Modules:
  0.0 43.5 jit_solution(4825416823178535414)
XLA Ops:
  0.6 41.1 %exchange.1 = (bf16[4,272,256]{2,1,0:T(8,128)(2,1)S(1)}, bf16[10,272,128]{2,1,0:T(8,128)(2,1)S(1)}) custom-call(s32[8]{0:T(128)} %counts_ref.3, bf16[128,8192]{1,0:T(8,128)(2,1)} %hidden_any.1, bf16[128,256]{1,0:T(8,128)(2,1)} %grad_any.1, s32[1,128]{1,0:T(1,128)} %bitcast.3, bf16[1088,256]{1,0:T(8,128)(2,1)} %quant_any.1, f32[2,1088]{1,0:T(2,128)} %bitcast.2), custom_call_target="tpu_custom_call" | custom-call | tf_op jit(solution)/shard_map/exchange/pallas_call | solution.py:555
  41.7 1.8 %assemble.1 = (bf16[1088,256]{1,0:T(8,128)(2,1)}, bf16[128,2048]{1,0:T(8,128)(2,1)}) custom-call(s32[8]{0:T(128)} %counts_ref.3, bf16[10,272,128]{2,1,0:T(8,128)(2,1)S(1)} %get-tuple-element.4.pieces_ref, bf16[4,272,256]{2,1,0:T(8,128)(2,1)S(1)} %get-tuple-element.5.grad_ref), custom_call_target="tpu_custom_call" | custom-call | tf_op jit(solution)/shard_map/assemble/pallas_call | solution.py:602

commit v4 on v3

--- a/solution.py
+++ b/solution.py
@@ -16,10 +16,12 @@
 VMEM_LIMIT = 24 * 2**20
 SIDE_CORE = 1
 HIDE_AT = (1, 3)
-WEIGH_FROM = (2, 1)
+WEIGH_FROM = (3, 1)
 WEIGH_AT = 4
 OUT_AT = 5
 EARLY = 0
+FLUSH = -1
+BESIDE_AT = 3
 MESH = pl.DeviceIdType.MESH
 
 rope_base = 500000.0
@@ -120,7 +122,7 @@
     hidden_in, grad_ref, positions_ref, quant_ref, scales_ref,
     weights_ref, rotated, weights, picked, hidden, outgoing, grad_send,
     load_sem, w_send, w_recv, h_send, h_recv,
-    z_send, first_send, second_send, net_recv, pair_send, pair_recv,
+    z_send, end_send, first_send, second_send, net_recv, pair_send, pair_recv,
     o_send, b_send, e_send, o_recv, g_send, g_recv,
     column_in, beside_in,
 ):
@@ -267,7 +269,7 @@
     def own_row(level):
         return level * LINE + y, side
 
-    sideways = core == SIDE_CORE
+    sideways = core >= SIDE_CORE
 
     def first_row(level):
         return level * LINE + jnp.where(sideways, y, 1 - y), jnp.where(sideways, 1 - side, side)
@@ -316,6 +318,20 @@
                 def _():
                     act(sign, level)
 
+    def climb_inside(level, act):
+        @pl.when((level > 0) & (level < depth - 1))
+        def _():
+            act(climb(level))
+
+    def feed_ends(level, act):
+        @pl.when((z == 1) & (level > 1))
+        def _():
+            act(relay(*own_row(level), end_send.at[level], (y, part)))
+
+        @pl.when((z == depth - 2) & (level < depth - 2))
+        def _():
+            act(relay(*own_row(level), end_send.at[level], ((depth - 1) * LINE + y, part)))
+
     def tell(level, known):
         pl.semaphore_signal(
             column_in.at[known], inc=1, device_id=(level * LINE + y, part), device_id_type=MESH
@@ -333,7 +349,7 @@
     def farther(sign, level):
         pl.semaphore_wait(column_in.at[level], 1)
         heard(sign, level)
-        climb(level).start()
+        climb_inside(level, begin)
 
     for away in range(2, depth):
         at_levels(away, farther)
@@ -367,6 +383,7 @@
             pl.semaphore_wait(beside_in, 1)
             for away in range(1, depth):
                 at_levels(away, lambda sign, level: hide(level * LINE + 1 - y).start())
+        if stage == BESIDE_AT:
             hide(beside).start()
         for kind, at in enumerate(WEIGH_FROM):
             if stage == at:
@@ -411,6 +428,10 @@
     ready, made = [], []
     for stage in range(1, depth + 3):
 
+        def pass_z(sign, level):
+            feed_ends(level, begin)
+            from_z(level, begin)
+
         def take(name, row_of, pass_on):
             def act(sign, level):
                 with jax.named_scope(f"{name}{stage}{sign}"):
@@ -420,7 +441,7 @@
             return act
 
         if stage < depth:
-            at_levels(stage, take("z", own_row, lambda sign, level: from_z(level, begin)))
+            at_levels(stage, take("z", own_row, pass_z))
         at_levels(stage - 1, take("first", first_row, lambda sign, level: from_first(level, begin)))
         at_levels(stage - 1, take("second", second_row, lambda sign, level: from_second(level, begin)))
         at_levels(stage - 2, take("last", last_row, lambda sign, level: from_last(level, begin)))
@@ -445,7 +466,7 @@
                 made.append(due)
             ready = []
         if stage >= OUT_AT:
-            for away, row in made[::-1]:
+            for away, row in made[::FLUSH]:
                 at_levels(away, lambda sign, level, row=row: send_piece(level * LINE + row, begin))
             made = []
 
@@ -472,8 +493,12 @@
     for step in range(1, owners_n):
         hide(lax.rem(here + step, owners_n)).wait_send()
     for away in range(depth):
+        if away == 1:
+            at_levels(away, lambda sign, level: climb(level).wait_send())
+        if away > 1:
+            at_levels(away, lambda sign, level: climb_inside(level, finish))
         if away:
-            at_levels(away, lambda sign, level: climb(level).wait_send())
+            at_levels(away, lambda sign, level: feed_ends(level, finish))
         at_levels(away, lambda sign, level: from_z(level, finish))
         at_levels(away, lambda sign, level: from_first(level, finish))
         at_levels(away, lambda sign, level: from_second(level, finish))
@@ -576,7 +601,8 @@
             dma((4 + LOADS,)),
             dma((group_total - 1,)), dma((group_total - 1,)),
             dma((owners_n,)), dma((owners_n,)),
-            dma((owners_n // LINE,)), dma((owners_n,)), dma((2 * owners_n,)), dma((2 * owners_n,)),
+            dma((owners_n // LINE,)), dma((owners_n // LINE,)),
+            dma((owners_n,)), dma((2 * owners_n,)), dma((2 * owners_n,)),
             dma((2 * owners_n,)), dma((2 * owners_n,)),
             dma((owners_n,)), dma((owners_n,)), dma((2,)), dma((pieces_n,)),
             dma((group_total - 1,)), dma((group_total - 1,)),

time: 44 us -> 43.5 us (0.989)
  the two profiles are of different devices: /device:TPU:1 before, /device:TPU:11 now
where the time goes in v4:
time: 43.5 us; the launch traced here: 43.3 us
  Pallas kernels  42.7 us (98%)
  between operations  0.64 us (1%)
    pallas_call x1, Pallas kernels, exchange_plan(): pl.pallas_call(functools.partial(exchange_kernel, owners_n, group_total),...  40.9 us
    pallas_call x1, Pallas kernels, exchange_plan(): pl.pallas_call(functools.partial(assemble_kernel, owners_n, group_total,...  1.77 us

profile of v4, /device:TPU:11, one launch (start us, length us, event | category | flops | bytes accessed | tf_op | source)
XLA Modules:
  0.0 43.3 jit_solution(14653196696912901466)
XLA Ops:
  0.6 40.9 %exchange.1 = (bf16[4,272,256]{2,1,0:T(8,128)(2,1)S(1)}, bf16[10,272,128]{2,1,0:T(8,128)(2,1)S(1)}) custom-call(s32[8]{0:T(128)} %counts_ref.3, bf16[128,8192]{1,0:T(8,128)(2,1)} %hidden_any.1, bf16[128,256]{1,0:T(8,128)(2,1)} %grad_any.1, s32[1,128]{1,0:T(1,128)} %bitcast.3, bf16[1088,256]{1,0:T(8,128)(2,1)} %quant_any.1, f32[2,1088]{1,0:T(2,128)} %bitcast.2), custom_call_target="tpu_custom_call" | custom-call | tf_op jit(solution)/shard_map/exchange/pallas_call | solution.py:580
  41.6 1.8 %assemble.1 = (bf16[1088,256]{1,0:T(8,128)(2,1)}, bf16[128,2048]{1,0:T(8,128)(2,1)}) custom-call(s32[8]{0:T(128)} %counts_ref.3, bf16[10,272,128]{2,1,0:T(8,128)(2,1)S(1)} %get-tuple-element.4.pieces_ref, bf16[4,272,256]{2,1,0:T(8,128)(2,1)S(1)} %get-tuple-element.5.grad_ref), custom_call_target="tpu_custom_call" | custom-call | tf_op jit(solution)/shard_map/assemble/pallas_call | solution.py:628

commit v5 on v4

--- a/solution.py
+++ b/solution.py
@@ -474,18 +474,25 @@
         for step in range(1, owners_n):
             hidden_from(lax.rem(here + step, owners_n)).wait_recv()
 
-    def send_grad(kind):
+    upper = (quarter // 2 + 15) // 16 * 16
+    halves = (pl.ds(0, upper), pl.ds(upper, quarter - upper))
+
+    def send_grad(kind, half):
+        at, rows = kind * 2 + half, halves[half]
         return remote(
-            grad_send.at[peers[kind]], grad_out.at[part], g_send.at[kind], g_recv.at[kind], (here, peers[kind])
-        )
-
+            grad_send.at[peers[kind], rows, :], grad_out.at[part, rows, :], g_send.at[at], g_recv.at[at],
+            (here, peers[kind]),
+        )
+
+    pieces = [(kind, half) for kind in range(3) for half in range(2)]
     with jax.named_scope("reduce"):
-        for kind, target in enumerate(peers + (part,)):
-            grad_send[target] = jnp.dot(
-                hidden[...], rotated[:, cols_of(target)], preferred_element_type=jnp.float32
+        for step, (kind, half) in enumerate(pieces + [(3, 0), (3, 1)]):
+            target = (peers + (part,))[kind]
+            grad_send[target, halves[half], :] = jnp.dot(
+                hidden[halves[half], :], rotated[:, cols_of(target)], preferred_element_type=jnp.float32
             ).astype(jnp.bfloat16)
-            if kind:
-                send_grad(kind - 1).start()
+            if 0 < step <= len(pieces):
+                send_grad(*pieces[step - 1]).start()
     grad_out[part] = grad_send[part]
 
     for kind in range(3):
@@ -557,9 +564,9 @@
     for owner in range(owners_n):
         send_piece(jnp.int32(owner), finish)
     with jax.named_scope("grads"):
-        for kind in range(3):
-            send_grad(kind).wait_send()
-            remote(grad_send.at[0], grad_out.at[0], g_send.at[kind], g_recv.at[kind], (here, partner)).wait_recv()
+        for kind, half in pieces:
+            send_grad(kind, half).wait_send()
+            send_grad(kind, half).wait_recv()
 
 
 def exchange_plan(hidden_in, key_grad, positions, key_quant, key_scales, block_counts):
@@ -605,7 +612,7 @@
             dma((owners_n,)), dma((2 * owners_n,)), dma((2 * owners_n,)),
             dma((2 * owners_n,)), dma((2 * owners_n,)),
             dma((owners_n,)), dma((owners_n,)), dma((2,)), dma((pieces_n,)),
-            dma((group_total - 1,)), dma((group_total - 1,)),
+            dma((2 * group_total - 2,)), dma((2 * group_total - 2,)),
             pltpu.SemaphoreType.REGULAR((owners_n // LINE,)), pltpu.SemaphoreType.REGULAR,
         ],
         compiler_params=pltpu.CompilerParams(

time: 43.5 us -> 43.5 us (level)
  no operation moved by 1% of the time
where the time goes in v5:
time: 43.5 us; the launch traced here: 43.4 us
  Pallas kernels  42.7 us (98%)
  between operations  0.64 us (1%)
    pallas_call x1, Pallas kernels, exchange_plan(): pl.pallas_call(functools.partial(exchange_kernel, owners_n, group_total),...  41 us
    pallas_call x1, Pallas kernels, exchange_plan(): pl.pallas_call(functools.partial(assemble_kernel, owners_n, group_total,...  1.77 us

profile of v5, /device:TPU:11, one launch (start us, length us, event | category | flops | bytes accessed | tf_op | source)
XLA Modules:
  0.0 43.4 jit_solution(12502212841159455970)
XLA Ops:
  0.6 41.0 %exchange.1 = (bf16[4,272,256]{2,1,0:T(8,128)(2,1)S(1)}, bf16[10,272,128]{2,1,0:T(8,128)(2,1)S(1)}) custom-call(s32[8]{0:T(128)} %counts_ref.3, bf16[128,8192]{1,0:T(8,128)(2,1)} %hidden_any.1, bf16[128,256]{1,0:T(8,128)(2,1)} %grad_any.1, s32[1,128]{1,0:T(1,128)} %bitcast.3, bf16[1088,256]{1,0:T(8,128)(2,1)} %quant_any.1, f32[2,1088]{1,0:T(2,128)} %bitcast.2), custom_call_target="tpu_custom_call" | custom-call | tf_op jit(solution)/shard_map/exchange/pallas_call | solution.py:587
  41.6 1.8 %assemble.1 = (bf16[1088,256]{1,0:T(8,128)(2,1)}, bf16[128,2048]{1,0:T(8,128)(2,1)}) custom-call(s32[8]{0:T(128)} %counts_ref.3, bf16[10,272,128]{2,1,0:T(8,128)(2,1)S(1)} %get-tuple-element.4.pieces_ref, bf16[4,272,256]{2,1,0:T(8,128)(2,1)S(1)} %get-tuple-element.5.grad_ref), custom_call_target="tpu_custom_call" | custom-call | tf_op jit(solution)/shard_map/assemble/pallas_call | solution.py:635
